TPU v7x, 8 devices: a whole 2x2x1 slice. The times are simulated.
8 devices in a mesh: batch: 1 (over z), col: 2 (over y), row: 4 (over x, core).
Axes of the slice: x: 2, y: 2, z: 1, core: 2. Of those that a mesh axis runs over, the one named last changes fastest.
Arguments:
- lower_cyc: float32 [3072, 3072], P(('batch', 'row'), 'col')
Outputs:
- output: float32 [3072, 3072], P(('batch', 'row'), 'col')
All inputs are finite; a program needn't handle non-finite values.
Results may differ from a plain program's by a relative error of at most 0.001.
Values sent between devices are 32-bit elements.
A program may use at most 1 GiB of HBM per device.

v0:
```python
import jax
import jax.numpy as jnp
from jax import lax
from jax.sharding import PartitionSpec as P

DEPTH = 3
BLK = 8


def highest_matmul(left, right):
    return jnp.einsum("sik,skj->sij", left, right, precision=lax.Precision.HIGHEST, preferred_element_type=jnp.float32)


def natural_inner_cols(gathered):
    num_sub, row_len, grid_len, col_len = gathered.shape
    split_view = gathered.reshape(num_sub, row_len, grid_len, col_len // BLK, BLK)
    return split_view.transpose(0, 1, 3, 2, 4).reshape(num_sub, row_len, grid_len * col_len)


def natural_inner_rows(gathered):
    num_sub, grid_len, row_len, col_len = gathered.shape
    split_view = gathered.reshape(num_sub, grid_len, row_len // BLK, BLK, col_len)
    return split_view.transpose(0, 2, 1, 3, 4).reshape(num_sub, grid_len * row_len, col_len)


def cyclic_product(left, right):
    left_panel = natural_inner_cols(lax.all_gather(left, "col", axis=2))
    right_panel = natural_inner_rows(lax.all_gather(right, "row", axis=1))
    return highest_matmul(left_panel, right_panel)


def leaf_inverses(local_l, grid_rows, grid_cols):
    row_idx = lax.axis_index("row")
    col_idx = lax.axis_index("col")
    leaves = 2 ** DEPTH
    row_len = local_l.shape[0] // leaves
    col_len = local_l.shape[1] // leaves
    blocks4 = local_l.reshape(leaves, row_len, leaves, col_len)
    diag_blocks = jnp.stack([blocks4[leaf_idx, :, leaf_idx, :] for leaf_idx in range(leaves)])
    gathered = lax.all_gather(lax.all_gather(diag_blocks, "row", axis=1), "col", axis=3)
    leaf_size = grid_rows * row_len
    split_view = gathered.reshape(leaves, grid_rows, row_len // BLK, BLK, grid_cols, col_len // BLK, BLK)
    natural = split_view.transpose(0, 2, 1, 3, 5, 4, 6).reshape(leaves, leaf_size, leaf_size)
    piece_len = col_len // grid_rows
    local_cols = row_idx * piece_len + jnp.arange(piece_len)
    target_cols = (local_cols // BLK) * (grid_cols * BLK) + col_idx * BLK + local_cols % BLK
    identity_cols = (jnp.arange(leaf_size)[:, None] == target_cols[None, :]).astype(jnp.float32)
    rhs_batch = jnp.broadcast_to(identity_cols, (leaves, leaf_size, piece_len))
    solved = lax.linalg.triangular_solve(natural, rhs_batch, left_side=True, lower=True)
    parted = solved.reshape(leaves, row_len // BLK, grid_rows, BLK, piece_len)
    owned_rows = lax.all_to_all(parted, "row", 2, 4, tiled=True)
    return owned_rows.reshape(leaves, row_len, col_len)


def solution(mesh):
    grid_rows = mesh.shape["row"]
    grid_cols = mesh.shape["col"]
    block_spec = P(("batch", "row"), "col")

    def device_body(local_l):
        inverse = leaf_inverses(local_l, grid_rows, grid_cols)
        for level_idx in reversed(range(DEPTH)):
            num_sub = 2 ** level_idx
            half_rows = inverse.shape[1]
            half_cols = inverse.shape[2]
            paired_inv = inverse.reshape(num_sub, 2, half_rows, half_cols)
            inv_upper = paired_inv[:, 0]
            inv_lower = paired_inv[:, 1]
            blocks6 = local_l.reshape(num_sub, 2, half_rows, num_sub, 2, half_cols)
            coupling = jnp.stack([blocks6[sub_idx, 1, :, sub_idx, 0, :] for sub_idx in range(num_sub)])
            temp_prod = cyclic_product(coupling, inv_upper)
            off_diag = -cyclic_product(inv_lower, temp_prod)
            upper_rows = jnp.concatenate([inv_upper, jnp.zeros_like(inv_upper)], axis=2)
            lower_rows = jnp.concatenate([off_diag, inv_lower], axis=2)
            inverse = jnp.concatenate([upper_rows, lower_rows], axis=1)
        return inverse.reshape(local_l.shape)

    return jax.shard_map(device_body, mesh=mesh, in_specs=(block_spec,), out_specs=block_spec, check_vma=False)
```

profile of v0, /device:TPU:0, one launch (start us, length us, event | category | flops | bytes accessed | tf_op | source)
XLA Modules:
  0.0 959.2 jit_solution(2024236362548014666)
XLA Ops:
  6.5 7.2 reshape.154
  13.7 3.4 slice_bitcast_fusion.22
  19.4 28.4 %all-gather.30.cloned.1.call-done = f32[8,384,192]{2,0,1:T(8,128)} async-done(((f32[8,96,192]{2,0,1:T(8,128)}), f32[8,384,192]{2,0,1:T(8,128)}) %all-gather.30.cloned.1.call-update) | async-done | bytes 2359312 | tf_op jit(solution)/shard_map/all_gather | solution.py:40
  47.8 4.5 copy.167
  53.1 77.6 %all-gather.32.cloned.1.call-done = f32[8,4,96,384]{2,0,1,3:T(8,128)} async-done(((f32[8,4,96,192]{2,0,1,3:T(8,128)}), f32[8,4,96,384]{2,0,1,3:T(8,128)}) %all-gather.32.cloned.1.call-update) | async-done | bytes 4718608 | tf_op jit(solution)/shard_map/all_gather | solution.py:40
  130.7 6.1 copy.168
  136.8 46.4 %reshape.155 = f32[8,4,12,8,2,24,8]{6,5,4,3,2,1,0:T(8,128)} reshape(f32[8,4,96,384]{3,2,1,0:T(8,128)} %copy.168) | data formatting | bytes 9437184 | tf_op jit(solution)/shard_map/reshape | solution.py:42
  183.2 102.6 %copy.169 = f32[8,12,4,8,24,2,8]{6,5,4,3,2,1,0:T(2,128)} copy(f32[8,12,4,8,24,2,8]{6,4,5,3,1,2,0:T(8,128)} %bitcast.9) | data formatting | bytes 9437184 | tf_op jit(solution)/shard_map/transpose | solution.py:43
  285.8 98.9 %reshape.156 = f32[8,384,384]{2,1,0:T(8,128)} reshape(f32[8,12,4,8,24,2,8]{6,5,4,3,2,1,0:T(2,128)} %copy.169) | data formatting | bytes 9437184 | tf_op jit(solution)/shard_map/reshape | solution.py:43
  384.7 4.9 broadcast_select_fusion
  389.6 9.8 %while.1 = (s32[]{:T(128)}, f32[8,384,384]{2,1,0:T(8,128)}, s32[3,2]{0,1:T(2,128)S(1)}, f32[3,8,128,128]{3,2,0,1:T(8,128)S(1)}, s32[]{:T(128)}) while((s32[]{:T(128)}, f32[8,384,384]{2,1,0:T(8,128)}, s32[3,2]{0,1:T(2,128)S(1)}, f32[3,8,128,128]{3,2,0,1:T(8,128)S(1)}, s32[]{:T(128)}) %tuple.41), condition=%wide.while_cond, body=%wide.while_body.sunk | while | flops 2 | bytes 1048685 | solution.py:49
  399.4 236.0 %custom-call.3 = f32[8,3,128,128]{2,3,1,0:T(8,128)S(1)} custom-call(f32[8,3,128,128]{3,2,1,0:T(8,128)S(1)} %bitcast.214), custom_call_target="InvertDiagBlocksLowerTriangular" | custom-call | tf_op jit(solution)/shard_map/triangular_solve | solution.py:49
  643.8 12.1 %all_to_all.15 = f32[4,1,36864]{2,1,0:T(1,128)S(1)} all-to-all(f32[4,1,36864]{2,1,0:T(1,128)S(1)} %reshape.230), channel_id=1, replica_groups=mesh['batch'=1,'col'=2,'row'=4] {'row'}, dimensions={0} | all-to-all | bytes 1179648 | tf_op jit(solution)/shard_map/all_to_all | solution.py:51
  662.3 9.6 reshape.160
  674.0 11.9 %all-gather.3 = f32[4,96,384]{1,0,2:T(4,128)S(1)} all-gather(f32[4,96,192]{1,0,2:T(4,128)S(1)} %copy.185), channel_id=5, replica_groups=mesh['batch'=1,'col'=2,'row'=4] {'col'}, dimensions={2}, use_global_device_ids=true | all-gather | bytes 884736 | tf_op jit(solution)/shard_map/all_gather | solution.py:27
  690.0 6.6 reshape.170
  699.9 10.6 %all-gather.2 = f32[4,1,96,384]{2,0,1,3:T(4,128)S(1)} all-gather(f32[4,1,96,192]{2,0,1,3:T(4,128)S(1)} %copy.179), channel_id=4, replica_groups=mesh['batch'=1,'col'=2,'row'=4] {'col'}, dimensions={3}, use_global_device_ids=true | all-gather | bytes 884736 | tf_op jit(solution)/shard_map/all_gather | solution.py:27
  716.3 10.5 %all-gather.38.cloned.1.call-done = f32[2,192,768]{2,0,1:T(2,128)} async-done(((f32[2,192,384]{2,0,1:T(2,128)}), f32[2,192,768]{2,0,1:T(2,128)}) %all-gather.38.cloned.1.call-update) | async-done | bytes 1179664 | tf_op jit(solution)/shard_map/all_gather | solution.py:27
  728.6 20.5 %all-gather.26.cloned.1.call-done = f32[2,4,192,384]{3,2,0,1:T(8,128)} async-done(((f32[2,1,192,384]{3,2,0,1:T(8,128)}), f32[2,4,192,384]{3,2,0,1:T(8,128)}) %all-gather.26.cloned.1.call-update) | async-done | bytes 2359312 | tf_op jit(solution)/shard_map/all_gather | solution.py:28
  751.1 4.0 fusion.18
  755.1 6.6 reshape.182
  765.6 4.7 all-gather.36.cloned.1.call-done
  772.2 20.5 %all-gather.40.cloned.1.call-done = f32[2,768,384]{2,1,0:T(8,128)} async-done(((f32[2,192,384]{2,1,0:T(8,128)}), f32[2,768,384]{2,1,0:T(8,128)}) %all-gather.40.cloned.1.call-update) | async-done | bytes 2359312 | tf_op jit(solution)/shard_map/all_gather | solution.py:28
  794.7 3.2 convolution_negate_fusion.1
  800.9 26.5 %all-gather.44.cloned.1.call-done = f32[1,1,384,2,1,768]{5,2,4,1,0,3:T(8,128)} async-done(((f32[1,1,384,1,1,768]{5,2,4,1,0,3:T(8,128)}), f32[1,1,384,2,1,768]{5,2,4,1,0,3:T(8,128)}) %all-gather.44.cloned.1.call-update) | async-done | bytes 2359312 | tf_op jit(solution)/shard_map/all_gather | solution.py:27
  831.1 32.3 %all-gather.28.cloned.1.call-done = f32[1,4,384,768]{3,2,0,1:T(8,128)} async-done(((f32[1,1,384,768]{3,2,0,1:T(8,128)}), f32[1,4,384,768]{3,2,0,1:T(8,128)}) %all-gather.28.cloned.1.call-update) | async-done | bytes 4718608 | tf_op jit(solution)/shard_map/all_gather | solution.py:28
  863.4 3.1 copy.208
  866.5 8.6 convolution_bitcast_fusion
  875.1 22.9 %all-gather.42.cloned.1.call-done = f32[1,1,384,1536]{3,2,1,0:T(8,128)} async-done(((f32[1,1,384,768]{3,2,1,0:T(8,128)}), f32[1,1,384,1536]{3,2,1,0:T(8,128)}) %all-gather.42.cloned.1.call-update) | async-done | bytes 2359312 | tf_op jit(solution)/shard_map/all_gather | solution.py:27
  903.0 31.1 %all-gather.46.cloned.1.call-done = f32[1536,768]{0,1:T(8,128)} async-done(((f32[384,768]{0,1:T(8,128)}), f32[1536,768]{0,1:T(8,128)}) %all-gather.46.cloned.1.call-update) | async-done | bytes 4718608 | tf_op jit(solution)/shard_map/all_gather | solution.py:28
  934.0 6.2 copy.212
  943.3 6.1 fusion.2
  (99 shorter events, 71.5 us)
Async XLA Ops:
  6.5 41.3 %all-gather.30.cloned.1.call-start = ((), (), s32[]{:S(2)}) async-start(), calls=%async_computation.4 | async-start | bytes 3932160 | tf_op jit(solution)/shard_map/all_gather | solution.py:40
  19.4 111.3 %all-gather.32.cloned.1.call-start = ((), (), s32[]{:S(2)}) async-start(), calls=%async_computation.5 | async-start | bytes 9437184 | tf_op jit(solution)/shard_map/all_gather | solution.py:40
  52.3 633.7 %all-gather.24.cloned.1.call-start = ((), (), s32[]{:S(2)}) async-start(), calls=%async_computation.1 | async-start | bytes 1966080 | tf_op jit(solution)/shard_map/all_gather | solution.py:28
  662.2 48.4 %all-gather.34.cloned.1.call-start = ((), (), s32[]{:S(2)}) async-start(), calls=%async_computation.6 | async-start | bytes 1966080 | tf_op jit(solution)/shard_map/all_gather | solution.py:28
  689.9 36.9 %all-gather.38.cloned.1.call-start = ((), (), s32[]{:S(2)}) async-start(), calls=%async_computation.8 | async-start | bytes 1769472 | tf_op jit(solution)/shard_map/all_gather | solution.py:27
  699.6 49.5 %all-gather.26.cloned.1.call-start = ((), (), s32[]{:S(2)}) async-start(), calls=%async_computation.2 | async-start | bytes 2949120 | tf_op jit(solution)/shard_map/all_gather | solution.py:28
  715.5 54.7 %all-gather.36.cloned.1.call-start = ((), (), s32[]{:S(2)}) async-start(), calls=%async_computation.7 | async-start | bytes 1769472 | tf_op jit(solution)/shard_map/all_gather | solution.py:27
  716.3 76.5 %all-gather.40.cloned.1.call-start = ((), (), s32[]{:S(2)}) async-start(), calls=%async_computation.9 | async-start | bytes 2949120 | tf_op jit(solution)/shard_map/all_gather | solution.py:28
  755.1 72.4 %all-gather.44.cloned.1.call-start = ((), (), s32[]{:S(2)}) async-start(), calls=%async_computation.11 | async-start | bytes 3538944 | tf_op jit(solution)/shard_map/all_gather | solution.py:27
  765.4 98.0 %all-gather.28.cloned.1.call-start = ((), (), s32[]{:S(2)}) async-start(), calls=%async_computation.3 | async-start | bytes 5898240 | tf_op jit(solution)/shard_map/all_gather | solution.py:28
  794.7 3.2 copy-start.2
  794.7 3.2 copy-start.3
  800.1 97.9 %all-gather.42.cloned.1.call-start = ((), (), s32[]{:S(2)}) async-start(), calls=%async_computation.10 | async-start | bytes 3538944 | tf_op jit(solution)/shard_map/all_gather | solution.py:27
  800.9 133.1 %all-gather.46.cloned.1.call-start = ((), (), s32[]{:S(2)}) async-start(), calls=%async_computation.12 | async-start | bytes 5898240 | tf_op jit(solution)/shard_map/all_gather | solution.py:28
  863.4 3.2 copy-start
  943.2 6.1 copy-start.1
Sparse Core Ops, SparseCore 0:
  19.5 28.2 all-gather.29
  52.4 78.2 all-gather.31
  662.4 15.7 all-gather.23
  690.0 15.7 all-gather.33
  707.1 19.5 all-gather.37
  728.1 20.8 all-gather.25
  750.6 19.6 all-gather.35
  771.8 20.9 all-gather.39
  794.3 33.1 all-gather.43
  828.8 34.5 all-gather.27
  864.9 33.1 all-gather.41
  899.4 34.5 all-gather.45
where the time goes:
time: 963 us; the launch traced here: 959 us
  local copies, waits for them, and re-layouts  353 us (37%)
  waiting for transfers between devices  277 us (29%)
  other arithmetic  248 us (26%)
  blocking collectives  34.5 us (4%)
  matrix products  31.7 us (3%)
  between operations  14.2 us (1%)
    another operation x5, other arithmetic, leaf_inverses(): lax.linalg.triangular_solve(natural, rhs_batch, left_side=True, lower=True)  241 us
    all_gather x6, waiting for transfers between devices, cyclic_product(): right_panel = natural_inner_rows(lax.all_gather(right, 'row', axis=1))  104 us
    transpose x1, local copies, waits for them, and re-layouts, leaf_inverses(): split_view.transpose(0, 2, 1, 3, 5, 4, 6)  103 us
    reshape x1, local copies, waits for them, and re-layouts, leaf_inverses(): split_view.transpose(0, 2, 1, 3, 5, 4, 6)  98.9 us
    all_gather x1, waiting for transfers between devices, leaf_inverses(): lax.all_gather(lax.all_gather(diag_blocks, 'row', axis=1), 'col', axis=3)  77.6 us
    all_gather x4, waiting for transfers between devices, cyclic_product(): left_panel = natural_inner_cols(lax.all_gather(left, 'col', axis=2))  64.6 us
    reshape x1, local copies, waits for them, and re-layouts, leaf_inverses(): gathered.reshape(leaves, grid_rows, row_len // BLK, BLK, grid_cols, col_l...  46.4 us
    all_gather x1, waiting for transfers between devices, leaf_inverses(): lax.all_gather(diag_blocks, 'row', axis=1)  28.4 us
  transfers between devices with their start and end apart: 12, of which 10 were waited for; matrix products, arithmetic and copies ran while one was open for 8% of the time, Pallas kernels for 0%

commit v1 on v0

v1 whole, which is shorter than its diff:
```python
import functools

import jax
import jax.numpy as jnp
from jax import lax
from jax.experimental import pallas as pl
from jax.experimental.pallas import tpu as pltpu
from jax.sharding import PartitionSpec as P

MESH = pl.DeviceIdType.MESH
F32 = jnp.float32

DIAG = [(i, i) for i in range(12)]
OFF_A = [(i, j) for i in range(1, 6) for j in range(i)]
OFF_B = [(i + 6, j + 6) for i in range(1, 6) for j in range(i)]
TILES = DIAG + OFF_A + OFF_B
TIDX = {ij: t for t, ij in enumerate(TILES)}
CHUNKS = [(0, 6), (6, 12), (12, 18), (18, 22), (22, 27), (27, 33), (33, 37), (37, 42)]
NC = len(CHUNKS)
NF, NG, ND, SO, SF, SG, SD = range(7)
W, T2, JW, HW = 128, 256, 384, 768


def dot(a, b):
    return jnp.dot(a, b, precision=lax.Precision.HIGHEST, preferred_element_type=F32)


def kernel(l_hbm, out, lt, c0, xa, xb, bx, tt, db, oa, xc, oc, zz, acc, ys,
           loc, snd, rcv, csnd, crcv, tsnd, trcv, osnd, orcv, misc_s, misc_r, osem, bar_dummy):
    del bar_dummy
    row = lax.axis_index("row")
    y = lax.axis_index("col")
    x = row // 2
    k = row % 2
    ox, ok, oy = 1 - x, 1 - k, 1 - y
    fid = {"row": row + (1 - k) * 2 * (1 - 2 * x), "col": y + k * (1 - 2 * y)}
    gid = {"row": row + k * 2 * (1 - 2 * x), "col": y + (1 - k) * (1 - 2 * y)}
    sid = {"row": 2 * x + ok, "col": y}
    xid = {"row": 2 * ox + k, "col": y}
    yid = {"row": row, "col": oy}
    fx, fy = x + (1 - k) * (1 - 2 * x), y + k * (1 - 2 * y)
    gx, gy = x + k * (1 - 2 * x), y + (1 - k) * (1 - 2 * y)

    started = []

    def remote(src, dst, ss, rs, dev):
        cp = pltpu.make_async_remote_copy(src_ref=src, dst_ref=dst, send_sem=ss, recv_sem=rs,
                                          device_id=dev, device_id_type=MESH)
        return cp

    def piece(c, q, p, xs):
        a, b = CHUNKS[c]
        return lt.at[a:b, q, p, :, xs, :, :]

    def put(c, kind, q, xs, dev):
        ref = piece(c, q, k, xs)
        cp = remote(ref, ref, snd.at[c, kind], rcv.at[c, kind], dev)
        cp.start()
        started.append(cp)

    def got(c, kind, q, p, xs):
        ref = piece(c, q, p, xs)
        remote(ref, ref, snd.at[c, kind], rcv.at[c, kind], sid).wait_recv()

    def local_copies(c):
        a, b = CHUNKS[c]
        return [pltpu.make_async_copy(l_hbm.at[8 * i:8 * i + 8, :, W * j:W * j + W],
                                      lt.at[a + n, y, k, :, x, :, :], loc.at[a + n])
                for n, (i, j) in enumerate(TILES[a:b])]

    for c in range(NC):
        for cp in local_copies(c):
            cp.start()
    c0own = c0.at[y, k]
    c0load = pltpu.make_async_copy(l_hbm.at[48:96, :, 0:HW], c0own, loc.at[42])
    c0load.start()

    barrier = pltpu.get_barrier_semaphore()
    for dev in (fid, gid, sid):
        pl.semaphore_signal(barrier, inc=1, device_id=dev, device_id_type=MESH)
    pl.semaphore_wait(barrier, 3)

    for c in range(NC):
        for cp in local_copies(c):
            cp.wait()
        put(c, NF, y, x, fid)
        if c < 2:
            put(c, NG, y, x, gid)
        put(c, SO, y, x, sid)

    c0load.wait()

    def cref(s, q, p):
        return c0.at[q, p, pl.ds(8 * s, 8)]

    def cput(s, kind, q, dev):
        ref = cref(s, q, k)
        return remote(ref, ref, csnd.at[s, kind], crcv.at[s, kind], dev)

    for s in range(6):
        cput(s, 1, y, sid).start()

    xa[...] = jnp.zeros(xa.shape, F32)
    xb[...] = jnp.zeros(xb.shape, F32)
    zz[...] = jnp.zeros(zz.shape, F32)

    def serve_f(c):
        got(c, NF, fy, k, fx)
        put(c, ND, fy, fx, gid)
        put(c, SF, fy, fx, sid)
        if c + 2 < NC:
            put(c + 2, NG, y, x, gid)

    def serve_g(c):
        got(c, NG, gy, k, gx)
        put(c, SG, gy, gx, sid)
        got(c, ND, oy, k, ox)
        put(c, SD, oy, ox, sid)

    def ready(c):
        got(c, SO, y, ok, x)
        got(c, SF, gy, ok, gx)
        got(c, SG, fy, ok, fx)
        got(c, SD, oy, ok, ox)

    serve_f(0)
    serve_f(1)
    serve_g(0)
    serve_g(1)
    serve_f(2)
    ready(0)
    ready(1)
    serve_f(3)

    lane = lax.broadcasted_iota(jnp.int32, (8, W), 1)
    grp = lane // 16
    G6 = 6
    sub = {}
    for p in range(2):
        for sg in range(2):
            for q in range(2):
                rows = []
                for g in range(G6):
                    v = jnp.zeros((8, W), F32)
                    for m in range(8):
                        v = jnp.where(grp == m, lt[2 * g + k, q, p, m, sg], v)
                    rows.append(v)
                sub[2 * sg + p, q] = jnp.concatenate(rows, axis=0)
    lane48 = lax.broadcasted_iota(jnp.int32, (8 * G6, W), 1)
    sub48 = lax.broadcasted_iota(jnp.int32, (8 * G6, W), 0) % 8
    base48 = (lane48 // 16) * 16
    yv = {}
    for be in range(4):
        for q in range(2):
            if be % 2 == q:
                yv[be, q] = jnp.where(lane48 % 16 == 8 * (be // 2) + sub48, 1.0, 0.0).astype(F32)
            else:
                yv[be, q] = jnp.zeros((8 * G6, W), F32)

    def rowcast(v, e):
        v3 = v.reshape(G6, 8, W)[:, e:e + 1, :]
        return jnp.broadcast_to(v3, (G6, 8, W)).reshape(8 * G6, W)

    for be in range(4):
        for e in range(8):
            idx = base48 + (8 * (be // 2) + e)
            gs = {b2: jnp.take_along_axis(sub[b2, be % 2], idx, axis=1, mode="promise_in_bounds")
                  for b2 in range(be, 4)}
            rinv = 1.0 / rowcast(gs[be], e)
            for q in range(2):
                piv = rowcast(yv[be, q], e) * rinv
                for b2 in range(be, 4):
                    new = yv[b2, q] - gs[b2] * piv
                    if b2 == be:
                        new = jnp.where(sub48 > e, new, jnp.where(sub48 == e, piv, yv[b2, q]))
                    yv[b2, q] = new
    for be in range(4):
        for q in range(2):
            ys[be, q] = yv[be, q].reshape(G6, 8, W)

    lane256 = lax.broadcasted_iota(jnp.int32, (8, T2), 1) % W

    def invert_some(g0, count):
        dd, ll = [], []
        for n in range(count):
            g = g0 + n
            rows = []
            for p in range(2):
                for m in range(8):
                    for sg in range(2):
                        parts = [jnp.where(grp == m, ys[2 * sg + p, q, g], 0.0) for q in range(2)]
                        rows.append(jnp.concatenate(parts, axis=1))
            dd.append(rows)
            ll.append([jnp.concatenate([lt[2 * g + k, q, p, m, sg] for q in range(2)], axis=1)
                       for p in range(2) for m in range(8) for sg in range(2)])
        for h8 in (2, 4, 8):
            odd = [b for b in range(32) if (b % 16) // h8 % 2 == 1]
            zero = jnp.zeros((8, T2), F32)
            tds = []
            for n in range(count):
                mo = [jnp.where(lane256 // (8 * h8) == (b % 16) // h8 - 1, ll[n][b], 0.0) for b in odd]
                tds.append(dot(jnp.concatenate(mo, axis=0), jnp.concatenate(dd[n], axis=0)))
            for n in range(count):
                tfull = [zero] * 32
                for o, b in enumerate(odd):
                    tfull[b] = tds[n][8 * o:8 * o + 8]
                xo = dot(jnp.concatenate([dd[n][b] for b in odd], axis=0), jnp.concatenate(tfull, axis=0))
                for o, b in enumerate(odd):
                    dd[n][b] = dd[n][b] - xo[8 * o:8 * o + 8]
        for n in range(count):
            db[g0 + n, k] = jnp.concatenate(dd[n], axis=0)

    def inv_body(it, carry):
        invert_some(3 * it, 3)
        return carry

    lax.fori_loop(0, 2, inv_body, 0)
    dbcopy = remote(db.at[:, k], db.at[:, k], misc_s.at[0], misc_r.at[0], sid)
    dbcopy.start()

    serve_f(4)
    serve_f(5)
    serve_g(2)
    ready(2)
    remote(db.at[:, ok], db.at[:, ok], misc_s.at[0], misc_r.at[0], sid).wait_recv()

    def ltile(t):
        return jnp.concatenate([lt[t, q].reshape(T2, W) for q in range(2)], axis=1)

    need = [0, 1, 1, 0, 0, 1]

    def place_a(i):
        @pl.when(k == need[i])
        def _():
            t = i // 2
            d = db[i // 2, i % 2, :, pl.ds(pl.multiple_of(y * W, W), W)]
            xa[i, :, :, :, :, W * t:W * t + W] = d.reshape(2, 8, 2, 8, W)

    def step_a(i):
        for j in range(i):
            n = W * (j // 2 + 1)
            d = dot(ltile(TIDX[i, j]), xa[j, :, :, :, :, 0:n].reshape(T2, n))
            n0 = 0 if j == 0 else W * ((j - 1) // 2 + 1)
            if n0:
                acc[:, 0:n0] = acc[:, 0:n0] + d[:, 0:n0]
            if n > n0:
                acc[:, n0:n] = d[:, n0:n]
        n = W * ((i + 1) // 2)
        r = -dot(db[i // 2, i % 2], acc[:, 0:n])
        xa[i, :, :, :, :, 0:n] = r.reshape(2, 8, 2, 8, n)
        place_a(i)

    def place_b(i):
        d = db[3 + i // 2, i % 2, :, pl.ds(pl.multiple_of(k * W, W), W)]
        xb[i, :, :, :, :, W * i:W * i + W] = d.reshape(2, 8, 2, 8, W)

    def step_b(i):
        for j in range(i):
            n = W * (j + 1)
            d = dot(ltile(TIDX[i + 6, j + 6]), xb[j, :, :, :, :, 0:n].reshape(T2, n))
            if j:
                acc[:, 0:n - W] = acc[:, 0:n - W] + d[:, 0:n - W]
            acc[:, n - W:n] = d[:, n - W:n]
        n = W * i
        r = -dot(db[3 + i // 2, i % 2], acc[:, 0:n])
        xb[i, :, :, :, :, 0:n] = r.reshape(2, 8, 2, 8, n)
        place_b(i)

    place_a(0)
    for i in (1, 2, 3):
        step_a(i)
    serve_f(6)
    serve_f(7)
    for s in range(6):
        cput(s, 0, y, yid).start()
    serve_g(3)
    ready(3)
    step_a(4)
    serve_g(4)
    ready(4)
    step_a(5)

    oacopy = remote(xa.at[:, ok, :, x, :, :], oa, misc_s.at[1], misc_r.at[1], sid)
    oacopy.start()

    outs = []

    def put_out(src, dst):
        cp = pltpu.make_async_copy(src, dst, osem.at[len(outs)])
        cp.start()
        outs.append(cp)

    def jcol(t, kk):
        return [kk, 3 - kk, 4 + kk][t]

    def lanes(t, kk):
        return pl.ds(pl.multiple_of(W * jcol(t, kk), W), W)

    for i in range(6):
        put_out(zz, out.at[i, :, :, HW:1536])
    for t in range(3):
        put_out(xa.at[:, k, :, x, :, W * t:W * t + W], out.at[0:6, :, :, lanes(t, k)])

    serve_g(5)
    ready(5)
    place_b(0)
    for i in (1, 2, 3):
        step_b(i)
    serve_g(6)
    ready(6)
    step_b(4)
    serve_g(7)
    ready(7)
    step_b(5)

    bxcopy = remote(xb.at[:, :, :, x, :, :], bx.at[k], misc_s.at[2], misc_r.at[2], sid)
    bxcopy.start()
    bxlocal = pltpu.make_async_copy(xb.at[:, :, :, x, :, :], bx.at[k], loc.at[43])
    bxlocal.start()

    def tput(s):
        ref = tt.at[s, :, :, x, :, :]
        return remote(ref, ref, tsnd.at[s], trcv.at[s], xid)

    def do_t(s):
        cput(s, 0, oy, yid).wait_recv()
        cput(s, 2, oy, sid).start()
        remote(cref(s, y, ok), cref(s, y, ok), csnd.at[s, 1], crcv.at[s, 1], sid).wait_recv()
        remote(cref(s, oy, ok), cref(s, oy, ok), csnd.at[s, 2], crcv.at[s, 2], sid).wait_recv()
        for u in range(3):
            n = W * (u + 1)
            parts = []
            for j in (2 * u, 2 * u + 1):
                for q in range(2):
                    parts.append(c0[q, :, pl.ds(8 * s, 8), :, W * j:W * j + W].reshape(W, W))
            rhs = jnp.concatenate([xa[2 * u + e, :, :, :, :, 0:n].reshape(T2, n) for e in range(2)], axis=0)
            d = dot(jnp.concatenate(parts, axis=1), rhs)
            if u:
                acc[0:W, 0:n - W] = acc[0:W, 0:n - W] + d[:, 0:n - W]
            acc[0:W, n - W:n] = d[:, n - W:n]
        tt[s, :, :, x, :, :] = acc[0:W, 0:JW].reshape(2, 8, 8, JW)
        tput(s).start()

    def do_x(s):
        ref = tt.at[s, :, :, ox, :, :]
        remote(ref, ref, tsnd.at[s], trcv.at[s], xid).wait_recv()
        acc[W:T2, 0:JW] = jnp.zeros((W, JW), F32)

        def body(u, carry):
            ln = pl.ds(pl.multiple_of(u * W, W), W)
            lhs = jnp.concatenate([bx[q, s, :, :, :, ln].reshape(W, W) for q in range(2)], axis=1)
            acc[W:T2, 0:JW] = acc[W:T2, 0:JW] - dot(lhs, tt[u].reshape(T2, JW))
            return carry

        lax.fori_loop(0, s + 1, body, 0)
        xc[s] = acc[W:T2, 0:JW].reshape(2, 8, 8, JW)
        remote(xc.at[s, ok], oc.at[s], osnd.at[s], orcv.at[s], sid).start()
        for t in range(3):
            put_out(xc.at[s, k, :, :, W * t:W * t + W], out.at[6 + s, :, :, lanes(t, k)])

    for s in range(8):
        if s < 6:
            do_t(s)
        if s == 1:
            bxlocal.wait()
            remote(bx.at[ok], bx.at[ok], misc_s.at[2], misc_r.at[2], sid).wait_recv()
            put_out(bx.at[y, :, k], out.at[6:12, :, :, HW:1536])
            remote(oa, oa, misc_s.at[1], misc_r.at[1], sid).wait_recv()
            for t in range(3):
                put_out(oa.at[:, :, :, W * t:W * t + W], out.at[0:6, :, :, lanes(t, ok)])
        if s >= 2:
            do_x(s - 2)
    for s in range(6):
        remote(oc.at[s], oc.at[s], osnd.at[s], orcv.at[s], sid).wait_recv()
        for t in range(3):
            put_out(oc.at[s, :, :, W * t:W * t + W], out.at[6 + s, :, :, lanes(t, ok)])

    for cp in started:
        cp.wait_send()
    for s in range(6):
        cput(s, 0, y, yid).wait_send()
        cput(s, 1, y, sid).wait_send()
        cput(s, 2, oy, sid).wait_send()
        tput(s).wait_send()
        remote(xc.at[s, ok], oc.at[s], osnd.at[s], orcv.at[s], sid).wait_send()
    dbcopy.wait_send()
    oacopy.wait_send()
    bxcopy.wait_send()
    for cp in outs:
        cp.wait()


def solution(mesh):
    spec = P(("batch", "row"), "col")
    vm = lambda *shape: pltpu.VMEM(shape, F32)
    dma = lambda *shape: pltpu.SemaphoreType.DMA(shape)

    def body(local_l):
        got = pl.pallas_call(
            kernel,
            name="tri_inverse",
            out_shape=jax.ShapeDtypeStruct((12, 8, 8, 1536), F32),
            in_specs=[pl.BlockSpec(memory_space=pl.ANY)],
            out_specs=pl.BlockSpec(memory_space=pl.ANY),
            scratch_shapes=[
                vm(42, 2, 2, 8, 2, 8, W),
                vm(2, 2, 48, 8, HW),
                vm(6, 2, 8, 2, 8, JW),
                vm(6, 2, 8, 2, 8, HW),
                vm(2, 6, 2, 8, 8, HW),
                vm(6, 2, 8, 2, 8, JW),
                vm(6, 2, T2, T2),
                vm(6, 8, 8, JW),
                vm(6, 2, 8, 8, JW),
                vm(6, 8, 8, JW),
                vm(8, 8, HW),
                vm(T2, HW),
                vm(4, 2, 6, 8, W),
                dma(44), dma(NC, 7), dma(NC, 7), dma(6, 3), dma(6, 3), dma(6), dma(6),
                dma(6), dma(6), dma(3), dma(3), dma(64), pltpu.SemaphoreType.REGULAR,
            ],
            compiler_params=pltpu.CompilerParams(
                collective_id=0, has_side_effects=True, vmem_limit_bytes=60 * 2**20),
        )(local_l.reshape(96, 8, 1536))
        return got.reshape(HW, 1536)

    return jax.shard_map(body, mesh=mesh, in_specs=(spec,), out_specs=spec, check_vma=False)
```

time: 963 us -> 106 us (0.11)
  local copies, waits for them, and re-layouts: 353 us -> 4.84 us
  waiting for transfers between devices: 277 us -> 0 us
  other arithmetic: 248 us -> 0 us
  Pallas kernels: 0 us -> 101 us
  blocking collectives: 34.5 us -> 0 us
  matrix products: 31.7 us -> 0 us
  between operations: 14.2 us -> 0.01 us
    all_gather x12 -> x0, waiting for transfers between devices: 275 us -> none  [the longest x6 104 us: cyclic_product(): right_panel = natural_inner_rows(lax.all_gather(right, 'row', axis=1))]
    another operation x7 -> x0, other arithmetic: 243 us -> none  [the longest x5 241 us: leaf_inverses(): lax.linalg.triangular_solve(natural, rhs_batch, left_side=True, lower=True)]
    reshape x10 -> x0, local copies, waits for them, and re-layouts: 181 us -> none  [the longest x1 98.9 us: leaf_inverses(): split_view.transpose(0, 2, 1, 3, 5, 4, 6)]
    transpose x10 -> x0, local copies, waits for them, and re-layouts: 115 us -> none  [the longest x1 103 us: leaf_inverses(): split_view.transpose(0, 2, 1, 3, 5, 4, 6)]
    pallas_call x0 -> x1, Pallas kernels: none -> 101 us  [body(): pl.pallas_call(kernel, name='tri_inverse', out_shape=jax.ShapeDtypeStruct...]
    dot_general x6 -> x0, matrix products: 25.5 us -> none  [highest_matmul(): jnp.einsum('sik,skj->sij', left, right, precision=lax.Precision.HIGHEST,...]
    all_gather x9 -> x0, local copies, waits for them, and re-layouts: 25.4 us -> none  [the longest x6 8.54 us: cyclic_product(): left_panel = natural_inner_cols(lax.all_gather(left, 'col', axis=2))]
    all_gather x2 -> x0, blocking collectives: 22.4 us -> none  [cyclic_product(): left_panel = natural_inner_cols(lax.all_gather(left, 'col', axis=2))]
  transfers between devices with their start and end apart: 12 -> 0, of which waited for: 10 -> 0; matrix products, arithmetic and copies ran while one was open for 8% -> 0% of each run, Pallas kernels for 0% -> 0%
where the time goes in v1:
time: 106 us
  Pallas kernels  101 us (95%)
  local copies, waits for them, and re-layouts  4.84 us (5%)
    pallas_call x1, Pallas kernels, body(): pl.pallas_call(kernel, name='tri_inverse', out_shape=jax.ShapeDtypeStruct...  101 us
    unnamed x1, local copies, waits for them, and re-layouts  4.84 us

profile of v1, /device:TPU:0, one launch (start us, length us, event | category | flops | bytes accessed | tf_op | source)
XLA Modules:
  0.0 105.7 jit_solution(14088159332418494176)
XLA Ops:
  0.0 100.8 %tri_inverse.1 = f32[12,8,8,1536]{3,2,1,0:T(8,128)} custom-call(f32[96,8,1536]{2,1,0:T(8,128)} %bitcast.3), custom_call_target="tpu_custom_call" | custom-call | tf_op jit(solution)/shard_map/tri_inverse/pallas_call | solution.py:399
  100.8 4.8 %copy.3 = f32[768,1536]{1,0:T(8,128)} copy(f32[768,1536]{1,0:T(8,128)} %bitcast.2) | data formatting | bytes 9437184

commit v2 on v1

v2 whole, which is shorter than its diff:
```python
import functools

import jax
import jax.numpy as jnp
from jax import lax
from jax.experimental import pallas as pl
from jax.experimental.pallas import tpu as pltpu
from jax.sharding import PartitionSpec as P

MESH = pl.DeviceIdType.MESH
F32 = jnp.float32

DIAG = [(i, i) for i in range(12)]
OFF_A = [(i, j) for i in range(1, 6) for j in range(i)]
OFF_B = [(i + 6, j + 6) for i in range(1, 6) for j in range(i)]
TILES = DIAG[:6] + OFF_A + DIAG[6:] + OFF_B
TIDX = {ij: t for t, ij in enumerate(TILES)}
CHUNKS = [(0, 6), (6, 12), (12, 16), (16, 21), (21, 27), (27, 33), (33, 37), (37, 42)]
NC = len(CHUNKS)
NF, NG, ND, SO, SF, SG, SD = range(7)
CP = [(0, 0, 8), (1, 0, 8), (2, 0, 8), (3, 0, 8), (4, 0, 8), (5, 0, 4), (5, 4, 8)]
NP = len(CP)
ORDER = [
    "g0 f3 f0 f4", "f1 g4 c3 g1", "f2 F3 F0 F4", "G4 F2 G0 C5", "D0 F1 f5 R0", "I0 C1 g3 c2",
    "G1 D4 g2 D1", "F5 C0 c1 R4", "c5 I1 Q0 f6", "C6 R1 D3 D2", "c6 A1 G2 c0", "g5 C3 A2 G3",
    "f7 R2 A3 c4", "C2 A4 R3 V0", "D5 A5 C4 F6", "a V1 T0 G5", "V2 g6 Q1 g7", "T1 V3 T2 S0",
    "R5 B1 B2 V4", "V5 T3 V6 X0", "T4 B3 X1 F7", "D6 G6 T5 T6", "Y0 G7 R6 X2", "B4 D7 X3 R7",
    "B5 X4 Y2 o", "X5 Y4 Y1 Y3", "Y5",
]
MODES = [0, 2, 0, 2, 2, 2, 3, 3]
W, T2, JW, HW = 128, 256, 384, 768


def dot(a, b):
    return jnp.dot(a, b, precision=lax.Precision.HIGHEST, preferred_element_type=F32)


def kernel(l_hbm, out, lt, c0, xa, xb, bx, tt, db, oa, xc, oc, zz, acc, accx, ys,
           loc, snd, rcv, csnd, crcv, tsnd, trcv, osnd, orcv, bsnd, brcv, bloc, misc_s, misc_r, osem):
    row = lax.axis_index("row")
    y = lax.axis_index("col")
    x = row // 2
    k = row % 2
    ox, ok, oy = 1 - x, 1 - k, 1 - y
    sid = {"row": 2 * x + ok, "col": y}
    xid = {"row": 2 * ox + k, "col": y}
    yid = {"row": row, "col": oy}

    def way(c, core):
        return (core, 1 - core, 1, 0)[MODES[c]]

    def first(c):
        v = way(c, k)
        return {"row": row + (1 - v) * 2 * (1 - 2 * x), "col": y + v * (1 - 2 * y)}

    def second(c):
        v = 1 - way(c, k)
        return {"row": row + (1 - v) * 2 * (1 - 2 * x), "col": y + v * (1 - 2 * y)}

    def from_first(c, core):
        v = way(c, core)
        return y + v * (1 - 2 * y), x + (1 - v) * (1 - 2 * x)

    def from_second(c, core):
        v = 1 - way(c, core)
        return y + v * (1 - 2 * y), x + (1 - v) * (1 - 2 * x)

    started = []

    def remote(src, dst, ss, rs, dev):
        cp = pltpu.make_async_remote_copy(src_ref=src, dst_ref=dst, send_sem=ss, recv_sem=rs,
                                          device_id=dev, device_id_type=MESH)
        return cp

    def piece(c, q, p, xs):
        a, b = CHUNKS[c]
        return lt.at[a:b, q, p, :, xs, :, :]

    def put(c, kind, q, xs, dev):
        ref = piece(c, q, k, xs)
        cp = remote(ref, ref, snd.at[c, kind], rcv.at[c, kind], dev)
        cp.start()
        started.append(cp)

    def got(c, kind, q, p, xs):
        ref = piece(c, q, p, xs)
        remote(ref, ref, snd.at[c, kind], rcv.at[c, kind], sid).wait_recv()

    def local_copies(c):
        a, b = CHUNKS[c]
        return [pltpu.make_async_copy(l_hbm.at[8 * i:8 * i + 8, :, W * j:W * j + W],
                                      lt.at[a + n, y, k, :, x, :, :], loc.at[a + n])
                for n, (i, j) in enumerate(TILES[a:b])]

    barrier = pltpu.get_barrier_semaphore()
    for dev in (xid, yid, sid):
        pl.semaphore_signal(barrier, inc=1, device_id=dev, device_id_type=MESH)
    steps = [(name[0], int(name[1:] or 0)) for group in ORDER for name in group.split()]
    c0load = pltpu.make_async_copy(l_hbm.at[48:96, :, 0:HW], c0.at[y, k], loc.at[42])
    loads = {}
    for what, n in steps:
        if what in "fg" and n not in loads:
            loads[n] = local_copies(n)
            for cp in loads[n]:
                cp.start()
        if what in "cC" and 42 not in loads:
            c0load.start()
            loads[42] = [c0load]
    pl.semaphore_wait(barrier, 3)

    def loaded(c):
        for cp in loads.pop(c, []):
            cp.wait()

    def own_first(c):
        loaded(c)
        put(c, NF, y, x, first(c))
        put(c, SO, y, x, sid)

    def own_second(c):
        loaded(c)
        put(c, NG, y, x, second(c))

    def cref(n, q, p):
        s, m0, m1 = CP[n]
        return c0.at[q, p, 8 * s + m0:8 * s + m1]

    def cput(n, kind, q, dev):
        ref = cref(n, q, k)
        return remote(ref, ref, csnd.at[n, kind], crcv.at[n, kind], dev)

    def cgot(n, kind, q, p):
        ref = cref(n, q, p)
        remote(ref, ref, csnd.at[n, kind], crcv.at[n, kind], sid).wait_recv()

    def clear():
        xa[...] = jnp.zeros(xa.shape, F32)
        xb[...] = jnp.zeros(xb.shape, F32)
        zz[...] = jnp.zeros(zz.shape, F32)

    def serve_f(c):
        q, xs = from_first(c, k)
        got(c, NF, q, k, xs)
        put(c, ND, q, xs, second(c))
        put(c, SF, q, xs, sid)

    def serve_g(c):
        q, xs = from_second(c, k)
        got(c, NG, q, k, xs)
        put(c, SG, q, xs, sid)

    def serve_d(c):
        got(c, ND, oy, k, ox)
        put(c, SD, oy, ox, sid)

    def ready(c):
        got(c, SO, y, ok, x)
        q, xs = from_first(c, ok)
        got(c, SF, q, ok, xs)
        q, xs = from_second(c, ok)
        got(c, SG, q, ok, xs)
        got(c, SD, oy, ok, ox)

    lane = lax.broadcasted_iota(jnp.int32, (8, W), 1)
    grp = lane // 16
    G6 = 3
    lane48 = lax.broadcasted_iota(jnp.int32, (8 * G6, W), 1)
    sub48 = lax.broadcasted_iota(jnp.int32, (8 * G6, W), 0) % 8
    base48 = (lane48 // 16) * 16
    def rowcast(v, e):
        v3 = v.reshape(G6, 8, W)[:, e:e + 1, :]
        return jnp.broadcast_to(v3, (G6, 8, W)).reshape(8 * G6, W)

    def dtile(half, g):
        return TIDX[6 * half, 6 * half] + 2 * g + k

    def substitute(half):
        sub = {}
        for p in range(2):
            for sg in range(2):
                for q in range(2):
                    rows = []
                    for g in range(G6):
                        v = jnp.zeros((8, W), F32)
                        for m in range(8):
                            v = jnp.where(grp == m, lt[dtile(half, g), q, p, m, sg], v)
                        rows.append(v)
                    sub[2 * sg + p, q] = jnp.concatenate(rows, axis=0)
        yv = {}
        for be in range(4):
            for q in range(2):
                if be % 2 == q:
                    yv[be, q] = jnp.where(lane48 % 16 == 8 * (be // 2) + sub48, 1.0, 0.0).astype(F32)
                else:
                    yv[be, q] = jnp.zeros((8 * G6, W), F32)

        for be in range(4):
            for e in range(8):
                idx = base48 + (8 * (be // 2) + e)
                gs = {b2: jnp.take_along_axis(sub[b2, be % 2], idx, axis=1, mode="promise_in_bounds")
                      for b2 in range(be, 4)}
                rinv = 1.0 / rowcast(gs[be], e)
                for q in range(2):
                    piv = rowcast(yv[be, q], e) * rinv
                    for b2 in range(be, 4):
                        new = yv[b2, q] - gs[b2] * piv
                        if b2 == be:
                            new = jnp.where(sub48 > e, new, jnp.where(sub48 == e, piv, yv[b2, q]))
                        yv[b2, q] = new
        for be in range(4):
            for q in range(2):
                ys[be, q] = yv[be, q].reshape(G6, 8, W)

    lane256 = lax.broadcasted_iota(jnp.int32, (8, T2), 1) % W

    def invert(half, count=G6):
        dd, ll = [], []
        for n in range(count):
            g = n
            rows = []
            for p in range(2):
                for m in range(8):
                    for sg in range(2):
                        parts = [jnp.where(grp == m, ys[2 * sg + p, q, g], 0.0) for q in range(2)]
                        rows.append(jnp.concatenate(parts, axis=1))
            dd.append(rows)
            ll.append([jnp.concatenate([lt[dtile(half, g), q, p, m, sg] for q in range(2)], axis=1)
                       for p in range(2) for m in range(8) for sg in range(2)])
        for h8 in (2, 4, 8):
            odd = [b for b in range(32) if (b % 16) // h8 % 2 == 1]
            zero = jnp.zeros((8, T2), F32)
            tds = []
            for n in range(count):
                mo = [jnp.where(lane256 // (8 * h8) == (b % 16) // h8 - 1, ll[n][b], 0.0) for b in odd]
                tds.append(dot(jnp.concatenate(mo, axis=0), jnp.concatenate(dd[n], axis=0)))
            for n in range(count):
                tfull = [zero] * 32
                for o, b in enumerate(odd):
                    tfull[b] = tds[n][8 * o:8 * o + 8]
                xo = dot(jnp.concatenate([dd[n][b] for b in odd], axis=0), jnp.concatenate(tfull, axis=0))
                for o, b in enumerate(odd):
                    dd[n][b] = dd[n][b] - xo[8 * o:8 * o + 8]
        for n in range(count):
            db[G6 * half + n, k] = jnp.concatenate(dd[n], axis=0)
        dbcopy(half, k).start()

    def dbcopy(half, kk):
        ref = db.at[G6 * half:G6 * half + G6, kk]
        return remote(ref, ref, misc_s.at[half], misc_r.at[half], sid)

    def ltile(t):
        return jnp.concatenate([lt[t, q].reshape(T2, W) for q in range(2)], axis=1)

    need = [0, 1, 1, 0, 0, 1]

    def place_a(i):
        @pl.when(k == need[i])
        def _():
            t = i // 2
            d = db[i // 2, i % 2, :, pl.ds(pl.multiple_of(y * W, W), W)]
            xa[i, :, :, :, :, W * t:W * t + W] = d.reshape(2, 8, 2, 8, W)

    def step_a(i):
        for j in range(i):
            n = W * (j // 2 + 1)
            d = dot(ltile(TIDX[i, j]), xa[j, :, :, :, :, 0:n].reshape(T2, n))
            n0 = 0 if j == 0 else W * ((j - 1) // 2 + 1)
            if n0:
                acc[:, 0:n0] = acc[:, 0:n0] + d[:, 0:n0]
            if n > n0:
                acc[:, n0:n] = d[:, n0:n]
        n = W * ((i + 1) // 2)
        r = -dot(db[i // 2, i % 2], acc[:, 0:n])
        xa[i, :, :, :, :, 0:n] = r.reshape(2, 8, 2, 8, n)
        place_a(i)

    def place_b(i):
        d = db[3 + i // 2, i % 2, :, pl.ds(pl.multiple_of(k * W, W), W)]
        xb[i, :, :, :, :, W * i:W * i + W] = d.reshape(2, 8, 2, 8, W)

    def step_b(i):
        for j in range(i):
            n = W * (j + 1)
            d = dot(ltile(TIDX[i + 6, j + 6]), xb[j, :, :, :, :, 0:n].reshape(T2, n))
            if j:
                acc[:, 0:n - W] = acc[:, 0:n - W] + d[:, 0:n - W]
            acc[:, n - W:n] = d[:, n - W:n]
        n = W * i
        r = -dot(db[3 + i // 2, i % 2], acc[:, 0:n])
        xb[i, :, :, :, :, 0:n] = r.reshape(2, 8, 2, 8, n)
        place_b(i)

    outs = []

    def put_out(src, dst):
        cp = pltpu.make_async_copy(src, dst, osem.at[len(outs)])
        cp.start()
        outs.append(cp)

    def jcol(t, kk):
        return [kk, 3 - kk, 4 + kk][t]

    def lanes(t, kk):
        return pl.ds(pl.multiple_of(W * jcol(t, kk), W), W)

    oacopy = remote(xa.at[:, ok, :, x, :, :], oa, misc_s.at[2], misc_r.at[2], sid)

    def finish_a():
        oacopy.start()
        for i in range(6):
            put_out(zz, out.at[i, :, :, HW:2 * HW])
        for t in range(3):
            put_out(xa.at[:, k, :, x, :, W * t:W * t + W], out.at[0:6, :, :, lanes(t, k)])

    def finish_oa():
        remote(oa, oa, misc_s.at[2], misc_r.at[2], sid).wait_recv()
        for t in range(3):
            put_out(oa.at[:, :, :, W * t:W * t + W], out.at[0:6, :, :, lanes(t, ok)])

    def bxcopy(i, kk):
        return remote(xb.at[i, :, :, x, :, :], bx.at[kk, i], bsnd.at[i], brcv.at[i], sid)

    def bxlocal(i):
        return pltpu.make_async_copy(xb.at[i, :, :, x, :, :], bx.at[k, i], bloc.at[i])

    def send_b(i):
        bxcopy(i, k).start()
        bxlocal(i).start()

    def get_b(i):
        bxlocal(i).wait()
        bxcopy(i, ok).wait_recv()
        put_out(bx.at[y, i, k], out.at[6 + i, :, :, HW:2 * HW])

    def tcopy(n, xs):
        s, m0, m1 = CP[n]
        ref = tt.at[s, :, m0:m1, xs, :, :]
        return remote(ref, ref, tsnd.at[n], trcv.at[n], xid)

    def serve_c(n):
        cgot(n, 0, oy, k)
        cput(n, 2, oy, sid).start()

    def do_t(n):
        s, m0, m1 = CP[n]
        g = 8 * (m1 - m0)
        cgot(n, 1, y, ok)
        cgot(n, 2, oy, ok)
        for u in range(3):
            w = W * (u + 1)
            parts = []
            for j in (2 * u, 2 * u + 1):
                for q in range(2):
                    parts.append(c0[q, :, 8 * s + m0:8 * s + m1, :, W * j:W * j + W].reshape(2 * g, W))
            rhs = jnp.concatenate([xa[2 * u + e, :, :, :, :, 0:w].reshape(T2, w) for e in range(2)], axis=0)
            d = dot(jnp.concatenate(parts, axis=1), rhs)
            if u:
                acc[0:2 * g, 0:w - W] = acc[0:2 * g, 0:w - W] + d[:, 0:w - W]
            acc[0:2 * g, w - W:w] = d[:, w - W:w]
        tt[s, :, m0:m1, x, :, :] = acc[0:2 * g, 0:JW].reshape(2, m1 - m0, 8, JW)
        tcopy(n, x).start()

    def xpart(s, u):
        ln = pl.ds(pl.multiple_of(u * W, W), W)
        lhs = jnp.concatenate([bx[q, s, :, :, :, ln].reshape(W, W) for q in range(2)], axis=1)
        return dot(lhs, tt[u].reshape(T2, JW))

    def do_x(s):
        get_b(s)
        accx[...] = jnp.zeros((W, JW), F32)

        def body(u, carry):
            accx[...] = accx[...] - xpart(s, u)
            return carry

        lax.fori_loop(0, s, body, 0)
        for n in range(NP):
            if CP[n][0] == s:
                tcopy(n, ox).wait_recv()
        xc[s] = (accx[...] - xpart(s, s)).reshape(2, 8, 8, JW)
        remote(xc.at[s, ok], oc.at[s], osnd.at[s], orcv.at[s], sid).start()
        for t in range(3):
            put_out(xc.at[s, k, :, :, W * t:W * t + W], out.at[6 + s, :, :, lanes(t, k)])

    def finish_x(s):
        remote(oc.at[s], oc.at[s], osnd.at[s], orcv.at[s], sid).wait_recv()
        for t in range(3):
            put_out(oc.at[s, :, :, W * t:W * t + W], out.at[6 + s, :, :, lanes(t, ok)])

    def inv(half):
        substitute(half)
        invert(half)

    def get_d(half):
        dbcopy(half, ok).wait_recv()
        (place_b if half else place_a)(0)

    def do_b(i):
        step_b(i)
        send_b(i)

    def csend(n):
        loaded(42)
        cput(n, 0, y, yid).start()

    def csib(n):
        loaded(42)
        cput(n, 1, y, sid).start()

    run = {"f": own_first, "g": own_second, "F": serve_f, "G": serve_g, "D": serve_d, "R": ready, "I": inv,
           "Q": get_d, "A": step_a, "B": do_b, "S": send_b, "C": csend, "c": csib, "V": serve_c, "T": do_t,
           "X": do_x, "Y": finish_x, "a": lambda _: finish_a(), "o": lambda _: finish_oa()}
    cleared = False
    for what, n in steps:
        if what in "FGDR" and not cleared:
            clear()
            cleared = True
        with jax.named_scope(f"{what}{n}"):
            run[what](n)

    for cp in started:
        cp.wait_send()
    for n in range(NP):
        cput(n, 0, y, yid).wait_send()
        cput(n, 1, y, sid).wait_send()
        cput(n, 2, oy, sid).wait_send()
        tcopy(n, x).wait_send()
    for s in range(6):
        bxcopy(s, k).wait_send()
        remote(xc.at[s, ok], oc.at[s], osnd.at[s], orcv.at[s], sid).wait_send()
    dbcopy(0, k).wait_send()
    dbcopy(1, k).wait_send()
    oacopy.wait_send()
    for cp in outs:
        cp.wait()


def solution(mesh):
    spec = P(("batch", "row"), "col")
    vm = lambda *shape: pltpu.VMEM(shape, F32)
    dma = lambda *shape: pltpu.SemaphoreType.DMA(shape)

    def body(local_l):
        got = pl.pallas_call(
            kernel,
            name="tri_inverse",
            out_shape=jax.ShapeDtypeStruct((12, 8, 8, 1536), F32),
            in_specs=[pl.BlockSpec(memory_space=pl.ANY)],
            out_specs=pl.BlockSpec(memory_space=pl.ANY),
            scratch_shapes=[
                vm(42, 2, 2, 8, 2, 8, W),
                vm(2, 2, 48, 8, HW),
                vm(6, 2, 8, 2, 8, JW),
                vm(6, 2, 8, 2, 8, HW),
                vm(2, 6, 2, 8, 8, HW),
                vm(6, 2, 8, 2, 8, JW),
                vm(6, 2, T2, T2),
                vm(6, 8, 8, JW),
                vm(6, 2, 8, 8, JW),
                vm(6, 8, 8, JW),
                vm(8, 8, HW),
                vm(T2, HW),
                vm(W, JW),
                vm(4, 2, 3, 8, W),
                dma(43), dma(NC, 7), dma(NC, 7), dma(NP, 3), dma(NP, 3), dma(NP), dma(NP),
                dma(6), dma(6), dma(6), dma(6), dma(6), dma(3), dma(3), dma(64),
            ],
            compiler_params=pltpu.CompilerParams(
                collective_id=0, has_side_effects=True, vmem_limit_bytes=47 * 2**20),
        )(local_l.reshape(96, 8, 1536))
        return got.reshape(HW, 1536)

    return jax.shard_map(body, mesh=mesh, in_specs=(spec,), out_specs=spec, check_vma=False)
```

time: 106 us -> 86.4 us (0.82)
  Pallas kernels: 101 us -> 84.1 us
  local copies, waits for them, and re-layouts: 4.84 us -> 2.19 us
    pallas_call x1, Pallas kernels: 101 us -> 84.1 us  [body(): pl.pallas_call(kernel, name='tri_inverse', out_shape=jax.ShapeDtypeStruct...]
    unnamed x1, local copies, waits for them, and re-layouts: 4.84 us -> 2.19 us
where the time goes in v2:
time: 86.4 us; the launch traced here: 86.3 us
  Pallas kernels  84.1 us (97%)
  local copies, waits for them, and re-layouts  2.19 us (3%)
    pallas_call x1, Pallas kernels, body(): pl.pallas_call(kernel, name='tri_inverse', out_shape=jax.ShapeDtypeStruct...  84.1 us
    unnamed x1, local copies, waits for them, and re-layouts  2.19 us

profile of v2, /device:TPU:0, one launch (start us, length us, event | category | flops | bytes accessed | tf_op | source)
XLA Modules:
  0.0 86.3 jit_solution(15658480328912761971)
XLA Ops:
  0.0 84.1 %tri_inverse.1 = f32[12,8,8,1536]{3,2,1,0:T(8,128)S(1)} custom-call(f32[96,8,1536]{2,1,0:T(8,128)} %bitcast.3), custom_call_target="tpu_custom_call" | custom-call | tf_op jit(solution)/shard_map/tri_inverse/pallas_call | solution.py:444
  84.1 2.2 %copy.3 = f32[768,1536]{1,0:T(8,128)} copy(f32[768,1536]{1,0:T(8,128)S(1)} %bitcast.2) | data formatting | bytes 9437184

commit v3 on v2

--- a/solution.py
+++ b/solution.py
@@ -20,12 +20,13 @@
 NF, NG, ND, SO, SF, SG, SD = range(7)
 CP = [(0, 0, 8), (1, 0, 8), (2, 0, 8), (3, 0, 8), (4, 0, 8), (5, 0, 4), (5, 4, 8)]
 NP = len(CP)
+TG = [(0, 1), (2, 3), (4,), (5,), (6,)]
 ORDER = [
     "g0 f3 f0 f4", "f1 g4 c3 g1", "f2 F3 F0 F4", "G4 F2 G0 C5", "D0 F1 f5 R0", "I0 C1 g3 c2",
     "G1 D4 g2 D1", "F5 C0 c1 R4", "c5 I1 Q0 f6", "C6 R1 D3 D2", "c6 A1 G2 c0", "g5 C3 A2 G3",
-    "f7 R2 A3 c4", "C2 A4 R3 V0", "D5 A5 C4 F6", "a V1 T0 G5", "V2 g6 Q1 g7", "T1 V3 T2 S0",
-    "R5 B1 B2 V4", "V5 T3 V6 X0", "T4 B3 X1 F7", "D6 G6 T5 T6", "Y0 G7 R6 X2", "B4 D7 X3 R7",
-    "B5 X4 Y2 o", "X5 Y4 Y1 Y3", "Y5",
+    "f7 R2 A3 c4", "C2 A4 R3 V0", "D5 A5 C4 F6", "a V1 G5 V2", "g6 Q1 g7 T0", "V3 S0 R5 B1",
+    "B2 V4 V5 T1", "V6 T2 B3 P0", "X0 X1 F7 D6", "G6 T3 T4 G7", "R6 B4 D7 P1", "X2 X3 R7 B5",
+    "o P2 X4 X5", "Y0 Y1 Y2 Y3", "Y4 Y5",
 ]
 MODES = [0, 2, 0, 2, 2, 2, 3, 3]
 W, T2, JW, HW = 128, 256, 384, 768
@@ -36,7 +37,7 @@
 
 
 def kernel(l_hbm, out, lt, c0, xa, xb, bx, tt, db, oa, xc, oc, zz, acc, accx, ys,
-           loc, snd, rcv, csnd, crcv, tsnd, trcv, osnd, orcv, bsnd, brcv, bloc, misc_s, misc_r, osem):
+           loc, snd, rcv, crcv, trcv, orcv, brcv, bloc, misc_r, osem):
     row = lax.axis_index("row")
     y = lax.axis_index("col")
     x = row // 2
@@ -78,25 +79,25 @@
 
     def put(c, kind, q, xs, dev):
         ref = piece(c, q, k, xs)
-        cp = remote(ref, ref, snd.at[c, kind], rcv.at[c, kind], dev)
+        cp = remote(ref, ref, snd.at[0], rcv.at[c, kind], dev)
         cp.start()
         started.append(cp)
 
     def got(c, kind, q, p, xs):
         ref = piece(c, q, p, xs)
-        remote(ref, ref, snd.at[c, kind], rcv.at[c, kind], sid).wait_recv()
+        remote(ref, ref, snd.at[0], rcv.at[c, kind], sid).wait_recv()
 
     def local_copies(c):
         a, b = CHUNKS[c]
         return [pltpu.make_async_copy(l_hbm.at[8 * i:8 * i + 8, :, W * j:W * j + W],
-                                      lt.at[a + n, y, k, :, x, :, :], loc.at[a + n])
+                                      lt.at[a + n, y, k, :, x, :, :], loc.at[c])
                 for n, (i, j) in enumerate(TILES[a:b])]
 
     barrier = pltpu.get_barrier_semaphore()
     for dev in (xid, yid, sid):
         pl.semaphore_signal(barrier, inc=1, device_id=dev, device_id_type=MESH)
     steps = [(name[0], int(name[1:] or 0)) for group in ORDER for name in group.split()]
-    c0load = pltpu.make_async_copy(l_hbm.at[48:96, :, 0:HW], c0.at[y, k], loc.at[42])
+    c0load = pltpu.make_async_copy(l_hbm.at[48:96, :, 0:HW], c0.at[y, k], loc.at[NC])
     loads = {}
     for what, n in steps:
         if what in "fg" and n not in loads:
@@ -127,11 +128,11 @@
 
     def cput(n, kind, q, dev):
         ref = cref(n, q, k)
-        return remote(ref, ref, csnd.at[n, kind], crcv.at[n, kind], dev)
+        return remote(ref, ref, snd.at[0], crcv.at[n, kind], dev)
 
     def cgot(n, kind, q, p):
         ref = cref(n, q, p)
-        remote(ref, ref, csnd.at[n, kind], crcv.at[n, kind], sid).wait_recv()
+        remote(ref, ref, snd.at[0], crcv.at[n, kind], sid).wait_recv()
 
     def clear():
         xa[...] = jnp.zeros(xa.shape, F32)
@@ -246,7 +247,7 @@
 
     def dbcopy(half, kk):
         ref = db.at[G6 * half:G6 * half + G6, kk]
-        return remote(ref, ref, misc_s.at[half], misc_r.at[half], sid)
+        return remote(ref, ref, snd.at[0], misc_r.at[half], sid)
 
     def ltile(t):
         return jnp.concatenate([lt[t, q].reshape(T2, W) for q in range(2)], axis=1)
@@ -293,7 +294,7 @@
     outs = []
 
     def put_out(src, dst):
-        cp = pltpu.make_async_copy(src, dst, osem.at[len(outs)])
+        cp = pltpu.make_async_copy(src, dst, osem.at[0])
         cp.start()
         outs.append(cp)
 
@@ -303,7 +304,7 @@
     def lanes(t, kk):
         return pl.ds(pl.multiple_of(W * jcol(t, kk), W), W)
 
-    oacopy = remote(xa.at[:, ok, :, x, :, :], oa, misc_s.at[2], misc_r.at[2], sid)
+    oacopy = remote(xa.at[:, ok, :, x, :, :], oa, snd.at[0], misc_r.at[2], sid)
 
     def finish_a():
         oacopy.start()
@@ -313,12 +314,12 @@
             put_out(xa.at[:, k, :, x, :, W * t:W * t + W], out.at[0:6, :, :, lanes(t, k)])
 
     def finish_oa():
-        remote(oa, oa, misc_s.at[2], misc_r.at[2], sid).wait_recv()
+        remote(oa, oa, snd.at[0], misc_r.at[2], sid).wait_recv()
         for t in range(3):
             put_out(oa.at[:, :, :, W * t:W * t + W], out.at[0:6, :, :, lanes(t, ok)])
 
     def bxcopy(i, kk):
-        return remote(xb.at[i, :, :, x, :, :], bx.at[kk, i], bsnd.at[i], brcv.at[i], sid)
+        return remote(xb.at[i, :, :, x, :, :], bx.at[kk, i], snd.at[0], brcv.at[i], sid)
 
     def bxlocal(i):
         return pltpu.make_async_copy(xb.at[i, :, :, x, :, :], bx.at[k, i], bloc.at[i])
@@ -335,55 +336,84 @@
     def tcopy(n, xs):
         s, m0, m1 = CP[n]
         ref = tt.at[s, :, m0:m1, xs, :, :]
-        return remote(ref, ref, tsnd.at[n], trcv.at[n], xid)
+        return remote(ref, ref, snd.at[0], trcv.at[n], xid)
 
     def serve_c(n):
         cgot(n, 0, oy, k)
         cput(n, 2, oy, sid).start()
 
-    def do_t(n):
-        s, m0, m1 = CP[n]
-        g = 8 * (m1 - m0)
-        cgot(n, 1, y, ok)
-        cgot(n, 2, oy, ok)
+    def do_t(h):
+        group = TG[h]
+        for n in group:
+            cgot(n, 1, y, ok)
+            cgot(n, 2, oy, ok)
+        lo = 8 * CP[group[0]][0] + CP[group[0]][1]
+        hi = 8 * CP[group[-1]][0] + CP[group[-1]][2]
+        g = 8 * (hi - lo)
         for u in range(3):
             w = W * (u + 1)
             parts = []
             for j in (2 * u, 2 * u + 1):
                 for q in range(2):
-                    parts.append(c0[q, :, 8 * s + m0:8 * s + m1, :, W * j:W * j + W].reshape(2 * g, W))
+                    parts.append(c0[q, :, lo:hi, :, W * j:W * j + W].reshape(2 * g, W))
             rhs = jnp.concatenate([xa[2 * u + e, :, :, :, :, 0:w].reshape(T2, w) for e in range(2)], axis=0)
             d = dot(jnp.concatenate(parts, axis=1), rhs)
             if u:
                 acc[0:2 * g, 0:w - W] = acc[0:2 * g, 0:w - W] + d[:, 0:w - W]
             acc[0:2 * g, w - W:w] = d[:, w - W:w]
-        tt[s, :, m0:m1, x, :, :] = acc[0:2 * g, 0:JW].reshape(2, m1 - m0, 8, JW)
-        tcopy(n, x).start()
-
-    def xpart(s, u):
-        ln = pl.ds(pl.multiple_of(u * W, W), W)
-        lhs = jnp.concatenate([bx[q, s, :, :, :, ln].reshape(W, W) for q in range(2)], axis=1)
-        return dot(lhs, tt[u].reshape(T2, JW))
-
-    def do_x(s):
-        get_b(s)
-        accx[...] = jnp.zeros((W, JW), F32)
-
-        def body(u, carry):
-            accx[...] = accx[...] - xpart(s, u)
-            return carry
-
-        lax.fori_loop(0, s, body, 0)
+        for n in group:
+            s, m0, m1 = CP[n]
+            at = 8 * (8 * s + m0 - lo)
+            size = 8 * (m1 - m0)
+            for p in range(2):
+                r = acc[p * g + at:p * g + at + size, 0:JW]
+                tt[s, p, m0:m1, x, :, :] = r.reshape(m1 - m0, 8, JW)
+            tcopy(n, x).start()
+
+    def tgot(s):
         for n in range(NP):
             if CP[n][0] == s:
                 tcopy(n, ox).wait_recv()
-        xc[s] = (accx[...] - xpart(s, s)).reshape(2, 8, 8, JW)
-        remote(xc.at[s, ok], oc.at[s], osnd.at[s], orcv.at[s], sid).start()
+
+    def bpart(s, count, u, nu):
+        parts = []
+        for e in range(nu):
+            ln = pl.ds(pl.multiple_of((u + e) * W, W), W)
+            for q in range(2):
+                parts.append(bx[q, s:s + count, :, :, :, ln].reshape(count * W, W))
+        rhs = jnp.concatenate([tt[u + e].reshape(T2, JW) for e in range(nu)], axis=0)
+        return dot(jnp.concatenate(parts, axis=1), rhs)
+
+    def do_p(a):
+        for s in (2 * a, 2 * a + 1):
+            get_b(s)
+
+        def body(it, carry):
+            accx[...] = accx[...] - bpart(2 * a, 2, 2 * it, 2)
+            return carry
+
+        if a > 1:
+            accx[...] = jnp.zeros((T2, JW), F32)
+            lax.fori_loop(0, a, body, 0)
+        elif a == 1:
+            accx[...] = -bpart(2, 2, 0, 2)
+
+    def do_x(s):
+        tgot(s)
+        if s == 0:
+            accx[...] = -bpart(0, 2, 0, 1)
+        elif s % 2 == 0:
+            accx[...] = accx[...] - bpart(s, 2, s, 1)
+        else:
+            accx[W:, :] = accx[W:, :] - bpart(s, 1, s, 1)
+        at = W * (s % 2)
+        xc[s] = accx[at:at + W, :].reshape(2, 8, 8, JW)
+        remote(xc.at[s, ok], oc.at[s], snd.at[0], orcv.at[s], sid).start()
         for t in range(3):
             put_out(xc.at[s, k, :, :, W * t:W * t + W], out.at[6 + s, :, :, lanes(t, k)])
 
     def finish_x(s):
-        remote(oc.at[s], oc.at[s], osnd.at[s], orcv.at[s], sid).wait_recv()
+        remote(oc.at[s], oc.at[s], snd.at[0], orcv.at[s], sid).wait_recv()
         for t in range(3):
             put_out(oc.at[s, :, :, W * t:W * t + W], out.at[6 + s, :, :, lanes(t, ok)])
 
@@ -409,7 +439,7 @@
 
     run = {"f": own_first, "g": own_second, "F": serve_f, "G": serve_g, "D": serve_d, "R": ready, "I": inv,
            "Q": get_d, "A": step_a, "B": do_b, "S": send_b, "C": csend, "c": csib, "V": serve_c, "T": do_t,
-           "X": do_x, "Y": finish_x, "a": lambda _: finish_a(), "o": lambda _: finish_oa()}
+           "X": do_x, "P": do_p, "Y": finish_x, "a": lambda _: finish_a(), "o": lambda _: finish_oa()}
     cleared = False
     for what, n in steps:
         if what in "FGDR" and not cleared:
@@ -427,7 +457,7 @@
         tcopy(n, x).wait_send()
     for s in range(6):
         bxcopy(s, k).wait_send()
-        remote(xc.at[s, ok], oc.at[s], osnd.at[s], orcv.at[s], sid).wait_send()
+        remote(xc.at[s, ok], oc.at[s], snd.at[0], orcv.at[s], sid).wait_send()
     dbcopy(0, k).wait_send()
     dbcopy(1, k).wait_send()
     oacopy.wait_send()
@@ -460,10 +490,9 @@
                 vm(6, 8, 8, JW),
                 vm(8, 8, HW),
                 vm(T2, HW),
-                vm(W, JW),
+                vm(T2, JW),
                 vm(4, 2, 3, 8, W),
-                dma(43), dma(NC, 7), dma(NC, 7), dma(NP, 3), dma(NP, 3), dma(NP), dma(NP),
-                dma(6), dma(6), dma(6), dma(6), dma(6), dma(3), dma(3), dma(64),
+                dma(NC + 1), dma(1), dma(NC, 7), dma(NP, 3), dma(NP), dma(6), dma(6), dma(6), dma(3), dma(1),
             ],
             compiler_params=pltpu.CompilerParams(
                 collective_id=0, has_side_effects=True, vmem_limit_bytes=47 * 2**20),

time: 86.4 us -> 87.5 us (1.013)
  Pallas kernels: 84.1 us -> 85.2 us
    pallas_call x1, Pallas kernels: 84.1 us -> 85.2 us  [body(): pl.pallas_call(kernel, name='tri_inverse', out_shape=jax.ShapeDtypeStruct...]
where the time goes in v3:
time: 87.5 us; the launch traced here: 87.4 us
  Pallas kernels  85.2 us (97%)
  local copies, waits for them, and re-layouts  2.19 us (3%)
    pallas_call x1, Pallas kernels, body(): pl.pallas_call(kernel, name='tri_inverse', out_shape=jax.ShapeDtypeStruct...  85.2 us
    unnamed x1, local copies, waits for them, and re-layouts  2.19 us

profile of v3, /device:TPU:0, one launch (start us, length us, event | category | flops | bytes accessed | tf_op | source)
XLA Modules:
  0.0 87.4 jit_solution(17766661706652376411)
XLA Ops:
  0.0 85.2 %tri_inverse.1 = f32[12,8,8,1536]{3,2,1,0:T(8,128)S(1)} custom-call(f32[96,8,1536]{2,1,0:T(8,128)} %bitcast.3), custom_call_target="tpu_custom_call" | custom-call | tf_op jit(solution)/shard_map/tri_inverse/pallas_call | solution.py:474
  85.2 2.2 %copy.3 = f32[768,1536]{1,0:T(8,128)} copy(f32[768,1536]{1,0:T(8,128)S(1)} %bitcast.2) | data formatting | bytes 9437184

commit v4 on v3

--- a/solution.py
+++ b/solution.py
@@ -10,25 +10,24 @@
 MESH = pl.DeviceIdType.MESH
 F32 = jnp.float32
 
-DIAG = [(i, i) for i in range(12)]
 OFF_A = [(i, j) for i in range(1, 6) for j in range(i)]
 OFF_B = [(i + 6, j + 6) for i in range(1, 6) for j in range(i)]
-TILES = DIAG[:6] + OFF_A + DIAG[6:] + OFF_B
+TILES = OFF_A + OFF_B
 TIDX = {ij: t for t, ij in enumerate(TILES)}
-CHUNKS = [(0, 6), (6, 12), (12, 16), (16, 21), (21, 27), (27, 33), (33, 37), (37, 42)]
+CHUNKS = [None, (0, 6), (6, 10), (10, 15), None, (15, 21), (21, 25), (25, 30)]
 NC = len(CHUNKS)
 NF, NG, ND, SO, SF, SG, SD = range(7)
 CP = [(0, 0, 8), (1, 0, 8), (2, 0, 8), (3, 0, 8), (4, 0, 8), (5, 0, 4), (5, 4, 8)]
 NP = len(CP)
 TG = [(0, 1), (2, 3), (4,), (5,), (6,)]
 ORDER = [
-    "g0 f3 f0 f4", "f1 g4 c3 g1", "f2 F3 F0 F4", "G4 F2 G0 C5", "D0 F1 f5 R0", "I0 C1 g3 c2",
-    "G1 D4 g2 D1", "F5 C0 c1 R4", "c5 I1 Q0 f6", "C6 R1 D3 D2", "c6 A1 G2 c0", "g5 C3 A2 G3",
-    "f7 R2 A3 c4", "C2 A4 R3 V0", "D5 A5 C4 F6", "a V1 G5 V2", "g6 Q1 g7 T0", "V3 S0 R5 B1",
-    "B2 V4 V5 T1", "V6 T2 B3 P0", "X0 X1 F7 D6", "G6 T3 T4 G7", "R6 B4 D7 P1", "X2 X3 R7 B5",
-    "o P2 X4 X5", "Y0 Y1 Y2 Y3", "Y4 Y5",
+    "f0 c5 g4 f3", "f4 g0 F3 f2", "f1 g2 G0 c4", "g1 F0 F4 F2", "f5 D0 f6 G1", "R0 D3 c0 c2",
+    "G2 F1 I0 g3", "C0 C1 c1 Q0", "D4 g5 g6 G4", "C2 D2 R4 R2", "D1 F5 F6 G3", "c6 C3 R1 I1",
+    "R3 A1 A2 V0", "A3 A4 V1 Q1", "G6 f7 A5 C4", "S0 G5 C5 T0", "c3 D5 V2 R5", "V3 B1 B2 C6",
+    "T1 V4 F7 B3", "D6 g7 P0 V5", "T2 X0 T3 V6", "X1 P1 Y0 R6", "B4 Y1 D7 T4", "G7 R7 B5 X2",
+    "X3 a0 P2 X4", "X5 o0 Y2 Y3", "Y4 Y5",
 ]
-MODES = [0, 2, 0, 2, 2, 2, 3, 3]
+MODES = [0, 0, 2, 1, 2, 2, 2, 3]
 W, T2, JW, HW = 128, 256, 384, 768
 
 
@@ -36,7 +35,7 @@
     return jnp.dot(a, b, precision=lax.Precision.HIGHEST, preferred_element_type=F32)
 
 
-def kernel(l_hbm, out, lt, c0, xa, xb, bx, tt, db, oa, xc, oc, zz, acc, accx, ys,
+def kernel(l_hbm, out, lt, ld, raw, c0, xa, xb, bx, tt, db, oa, xc, oc, zz, acc, accx, ys,
            loc, snd, rcv, crcv, trcv, orcv, brcv, bloc, misc_r, osem):
     row = lax.axis_index("row")
     y = lax.axis_index("col")
@@ -74,6 +73,8 @@
         return cp
 
     def piece(c, q, p, xs):
+        if CHUNKS[c] is None:
+            return ld.at[c // 4, q, p, :, :, xs, :, :]
         a, b = CHUNKS[c]
         return lt.at[a:b, q, p, :, xs, :, :]
 
@@ -88,6 +89,16 @@
         remote(ref, ref, snd.at[0], rcv.at[c, kind], sid).wait_recv()
 
     def local_copies(c):
+        if CHUNKS[c] is None:
+            h = c // 4
+            low, high = [], []
+            for n in range(6):
+                i = 6 * h + n
+                cols = slice(W * i, W * i + W)
+                low.append(pltpu.make_async_copy(l_hbm.at[8 * i:8 * i + 4, :, cols], raw.at[h, n], loc.at[c]))
+                high.append(pltpu.make_async_copy(l_hbm.at[8 * i + 4:8 * i + 8, :, cols],
+                                                  ld.at[h, y, k, n, :, x, :, :], loc.at[c]))
+            return low + high
         a, b = CHUNKS[c]
         return [pltpu.make_async_copy(l_hbm.at[8 * i:8 * i + 8, :, W * j:W * j + W],
                                       lt.at[a + n, y, k, :, x, :, :], loc.at[c])
@@ -104,14 +115,27 @@
             loads[n] = local_copies(n)
             for cp in loads[n]:
                 cp.start()
-        if what in "cC" and 42 not in loads:
+        if what in "cC" and NC not in loads:
             c0load.start()
-            loads[42] = [c0load]
+            loads[NC] = [c0load]
     pl.semaphore_wait(barrier, 3)
 
+    lane = lax.broadcasted_iota(jnp.int32, (8, W), 1)
+    grp = lane // 16
+
+    def turn(v):
+        return jnp.concatenate([v[:, W // 2:], v[:, :W // 2]], axis=1)
+
     def loaded(c):
-        for cp in loads.pop(c, []):
+        copies = loads.pop(c, [])
+        for cp in copies:
             cp.wait()
+        if copies and c < NC and CHUNKS[c] is None:
+            h = c // 4
+            for g in range(3):
+                for m in range(4):
+                    v = jnp.where(lane < W // 2, raw[h, 2 * g, m], turn(raw[h, 2 * g + 1, m]))
+                    ld[h, y, k, 6 + g, m, x] = v
 
     def own_first(c):
         loaded(c)
@@ -162,8 +186,6 @@
         got(c, SG, q, ok, xs)
         got(c, SD, oy, ok, ox)
 
-    lane = lax.broadcasted_iota(jnp.int32, (8, W), 1)
-    grp = lane // 16
     G6 = 3
     lane48 = lax.broadcasted_iota(jnp.int32, (8 * G6, W), 1)
     sub48 = lax.broadcasted_iota(jnp.int32, (8 * G6, W), 0) % 8
@@ -172,8 +194,11 @@
         v3 = v.reshape(G6, 8, W)[:, e:e + 1, :]
         return jnp.broadcast_to(v3, (G6, 8, W)).reshape(8 * G6, W)
 
-    def dtile(half, g):
-        return TIDX[6 * half, 6 * half] + 2 * g + k
+    def dl(half, g, q, p, m, sg):
+        if m >= 4:
+            return ld[half, q, p, 2 * g + k, m - 4, sg]
+        v = ld[half, q, p, 6 + g, m, sg]
+        return jnp.where(k == 1, turn(v), v)
 
     def substitute(half):
         sub = {}
@@ -184,7 +209,7 @@
                     for g in range(G6):
                         v = jnp.zeros((8, W), F32)
                         for m in range(8):
-                            v = jnp.where(grp == m, lt[dtile(half, g), q, p, m, sg], v)
+                            v = jnp.where(grp == m, dl(half, g, q, p, m, sg), v)
                         rows.append(v)
                     sub[2 * sg + p, q] = jnp.concatenate(rows, axis=0)
         yv = {}
@@ -225,7 +250,7 @@
                         parts = [jnp.where(grp == m, ys[2 * sg + p, q, g], 0.0) for q in range(2)]
                         rows.append(jnp.concatenate(parts, axis=1))
             dd.append(rows)
-            ll.append([jnp.concatenate([lt[dtile(half, g), q, p, m, sg] for q in range(2)], axis=1)
+            ll.append([jnp.concatenate([dl(half, g, q, p, m, sg) for q in range(2)], axis=1)
                        for p in range(2) for m in range(8) for sg in range(2)])
         for h8 in (2, 4, 8):
             odd = [b for b in range(32) if (b % 16) // h8 % 2 == 1]
@@ -430,11 +455,11 @@
         send_b(i)
 
     def csend(n):
-        loaded(42)
+        loaded(NC)
         cput(n, 0, y, yid).start()
 
     def csib(n):
-        loaded(42)
+        loaded(NC)
         cput(n, 1, y, sid).start()
 
     run = {"f": own_first, "g": own_second, "F": serve_f, "G": serve_g, "D": serve_d, "R": ready, "I": inv,
@@ -478,7 +503,9 @@
             in_specs=[pl.BlockSpec(memory_space=pl.ANY)],
             out_specs=pl.BlockSpec(memory_space=pl.ANY),
             scratch_shapes=[
-                vm(42, 2, 2, 8, 2, 8, W),
+                vm(30, 2, 2, 8, 2, 8, W),
+                vm(2, 2, 2, 9, 4, 2, 8, W),
+                vm(2, 6, 4, 8, W),
                 vm(2, 2, 48, 8, HW),
                 vm(6, 2, 8, 2, 8, JW),
                 vm(6, 2, 8, 2, 8, HW),

time: 87.5 us -> 81.2 us (0.928)
  Pallas kernels: 85.2 us -> 78.9 us
    pallas_call x1, Pallas kernels: 85.2 us -> 78.9 us  [body(): pl.pallas_call(kernel, name='tri_inverse', out_shape=jax.ShapeDtypeStruct...]
where the time goes in v4:
time: 81.2 us; the launch traced here: 81.1 us
  Pallas kernels  78.9 us (97%)
  local copies, waits for them, and re-layouts  2.19 us (3%)
    pallas_call x1, Pallas kernels, body(): pl.pallas_call(kernel, name='tri_inverse', out_shape=jax.ShapeDtypeStruct...  78.9 us
    unnamed x1, local copies, waits for them, and re-layouts  2.19 us

profile of v4, /device:TPU:0, one launch (start us, length us, event | category | flops | bytes accessed | tf_op | source)
XLA Modules:
  0.0 81.1 jit_solution(5989200952718532265)
XLA Ops:
  0.0 78.9 %tri_inverse.1 = f32[12,8,8,1536]{3,2,1,0:T(8,128)S(1)} custom-call(f32[96,8,1536]{2,1,0:T(8,128)} %bitcast.3), custom_call_target="tpu_custom_call" | custom-call | tf_op jit(solution)/shard_map/tri_inverse/pallas_call | solution.py:499
  78.9 2.2 %copy.3 = f32[768,1536]{1,0:T(8,128)} copy(f32[768,1536]{1,0:T(8,128)S(1)} %bitcast.2) | data formatting | bytes 9437184

commit v5 on v4

--- a/solution.py
+++ b/solution.py
@@ -16,19 +16,21 @@
 TIDX = {ij: t for t, ij in enumerate(TILES)}
 CHUNKS = [None, (0, 6), (6, 10), (10, 15), None, (15, 21), (21, 25), (25, 30)]
 NC = len(CHUNKS)
-NF, NG, ND, SO, SF, SG, SD = range(7)
+NF, NG, ND, SIB = range(4)
 CP = [(0, 0, 8), (1, 0, 8), (2, 0, 8), (3, 0, 8), (4, 0, 8), (5, 0, 4), (5, 4, 8)]
 NP = len(CP)
 TG = [(0, 1), (2, 3), (4,), (5,), (6,)]
 ORDER = [
-    "f0 c5 g4 f3", "f4 g0 F3 f2", "f1 g2 G0 c4", "g1 F0 F4 F2", "f5 D0 f6 G1", "R0 D3 c0 c2",
-    "G2 F1 I0 g3", "C0 C1 c1 Q0", "D4 g5 g6 G4", "C2 D2 R4 R2", "D1 F5 F6 G3", "c6 C3 R1 I1",
-    "R3 A1 A2 V0", "A3 A4 V1 Q1", "G6 f7 A5 C4", "S0 G5 C5 T0", "c3 D5 V2 R5", "V3 B1 B2 C6",
-    "T1 V4 F7 B3", "D6 g7 P0 V5", "T2 X0 T3 V6", "X1 P1 Y0 R6", "B4 Y1 D7 T4", "G7 R7 B5 X2",
-    "X3 a0 P2 X4", "X5 o0 Y2 Y3", "Y4 Y5",
+    "f1 f4 f0 f2", "g0 c3 C0 F4", "g1 F0 c2 G0", "g3 f3 g2 g4", "G1 D0 f5 c5", "R0 F1 c4 F2",
+    "g5 I0 D4 F3", "G4 D1 R4 c0", "g6 c1 I1 Q0", "G2 f6 C1 V0", "R1 D2 F5 Q1", "G5 G3 C2 A1",
+    "A2 A3 R2 D3", "R3 f7 S0 c6", "C3 F6 C4 G6", "A4 V1 A5 D5", "T0 V2 R5 F7", "a0 C5 B1 D6",
+    "B2 V3 T1 V4", "B3 P0 R6 g7", "X0 T2 X1 B4", "Y1 P1 D7 C6", "V5 G7 X2 T3", "R7 V6 B5 Y2",
+    "o0 T4 X3 P2", "X4 X5 Y0 Y4", "Y3 Y5",
 ]
-MODES = [0, 0, 2, 1, 2, 2, 2, 3]
+MODES = [2, 2, 3, 1, 1, 2, 2, 3]
 W, T2, JW, HW = 128, 256, 384, 768
+QW, HALF, SH = 32, 64, 24
+TWO = range(2)
 
 
 def dot(a, b):
@@ -74,7 +76,7 @@
 
     def piece(c, q, p, xs):
         if CHUNKS[c] is None:
-            return ld.at[c // 4, q, p, :, :, xs, :, :]
+            return ld.at[c // 4, q, p, :, xs, :, :]
         a, b = CHUNKS[c]
         return lt.at[a:b, q, p, :, xs, :, :]
 
@@ -95,9 +97,9 @@
             for n in range(6):
                 i = 6 * h + n
                 cols = slice(W * i, W * i + W)
-                low.append(pltpu.make_async_copy(l_hbm.at[8 * i:8 * i + 4, :, cols], raw.at[h, n], loc.at[c]))
-                high.append(pltpu.make_async_copy(l_hbm.at[8 * i + 4:8 * i + 8, :, cols],
-                                                  ld.at[h, y, k, n, :, x, :, :], loc.at[c]))
+                low.append(pltpu.make_async_copy(l_hbm.at[8 * i:8 * i + 6, :, cols], raw.at[h, n], loc.at[c]))
+                high.append(pltpu.make_async_copy(l_hbm.at[8 * i + 6:8 * i + 8, :, cols],
+                                                  ld.at[h, y, k, 4 * n + 2:4 * n + 4, x, :, :], loc.at[c]))
             return low + high
         a, b = CHUNKS[c]
         return [pltpu.make_async_copy(l_hbm.at[8 * i:8 * i + 8, :, W * j:W * j + W],
@@ -123,8 +125,8 @@
     lane = lax.broadcasted_iota(jnp.int32, (8, W), 1)
     grp = lane // 16
 
-    def turn(v):
-        return jnp.concatenate([v[:, W // 2:], v[:, :W // 2]], axis=1)
+    def turn(v, by):
+        return jnp.concatenate([v[:, by:], v[:, :by]], axis=1)
 
     def loaded(c):
         copies = loads.pop(c, [])
@@ -132,15 +134,19 @@
             cp.wait()
         if copies and c < NC and CHUNKS[c] is None:
             h = c // 4
+            for n in range(6):
+                for e in TWO:
+                    v = jnp.where(lane < W - QW, raw[h, n, 4 + e], turn(raw[h, n, e], QW))
+                    ld[h, y, k, 4 * n + e, x] = v
             for g in range(3):
-                for m in range(4):
-                    v = jnp.where(lane < W // 2, raw[h, 2 * g, m], turn(raw[h, 2 * g + 1, m]))
-                    ld[h, y, k, 6 + g, m, x] = v
+                for e in TWO:
+                    v = jnp.where(lane < HALF, raw[h, 2 * g, 2 + e], turn(raw[h, 2 * g + 1, 2 + e], HALF))
+                    ld[h, y, k, SH + 2 * g + e, x] = v
 
     def own_first(c):
         loaded(c)
         put(c, NF, y, x, first(c))
-        put(c, SO, y, x, sid)
+        put(c, SIB, y, x, sid)
 
     def own_second(c):
         loaded(c)
@@ -167,24 +173,24 @@
         q, xs = from_first(c, k)
         got(c, NF, q, k, xs)
         put(c, ND, q, xs, second(c))
-        put(c, SF, q, xs, sid)
+        put(c, SIB, q, xs, sid)
 
     def serve_g(c):
         q, xs = from_second(c, k)
         got(c, NG, q, k, xs)
-        put(c, SG, q, xs, sid)
+        put(c, SIB, q, xs, sid)
 
     def serve_d(c):
         got(c, ND, oy, k, ox)
-        put(c, SD, oy, ox, sid)
+        put(c, SIB, oy, ox, sid)
 
     def ready(c):
-        got(c, SO, y, ok, x)
-        q, xs = from_first(c, ok)
-        got(c, SF, q, ok, xs)
-        q, xs = from_second(c, ok)
-        got(c, SG, q, ok, xs)
-        got(c, SD, oy, ok, ox)
+        if CHUNKS[c] is None:
+            ref = ld.at[c // 4, :, ok]
+        else:
+            lo, hi = CHUNKS[c]
+            ref = lt.at[lo:hi, :, ok]
+        remote(ref, ref, snd.at[0], rcv.at[c, SIB], sid).wait_recv()
 
     G6 = 3
     lane48 = lax.broadcasted_iota(jnp.int32, (8 * G6, W), 1)
@@ -195,16 +201,19 @@
         return jnp.broadcast_to(v3, (G6, 8, W)).reshape(8 * G6, W)
 
     def dl(half, g, q, p, m, sg):
+        at = 4 * (2 * g + k)
         if m >= 4:
-            return ld[half, q, p, 2 * g + k, m - 4, sg]
-        v = ld[half, q, p, 6 + g, m, sg]
-        return jnp.where(k == 1, turn(v), v)
+            return ld[half, q, p, at + m - 4, sg]
+        if m < 2:
+            return turn(ld[half, q, p, at + m, sg], W - QW)
+        v = ld[half, q, p, SH + 2 * g + m - 2, sg]
+        return jnp.where(k == 1, turn(v, HALF), v)
 
     def substitute(half):
         sub = {}
-        for p in range(2):
-            for sg in range(2):
-                for q in range(2):
+        for p in TWO:
+            for sg in TWO:
+                for q in TWO:
                     rows = []
                     for g in range(G6):
                         v = jnp.zeros((8, W), F32)
@@ -214,7 +223,7 @@
                     sub[2 * sg + p, q] = jnp.concatenate(rows, axis=0)
         yv = {}
         for be in range(4):
-            for q in range(2):
+            for q in TWO:
                 if be % 2 == q:
                     yv[be, q] = jnp.where(lane48 % 16 == 8 * (be // 2) + sub48, 1.0, 0.0).astype(F32)
                 else:
@@ -226,7 +235,7 @@
                 gs = {b2: jnp.take_along_axis(sub[b2, be % 2], idx, axis=1, mode="promise_in_bounds")
                       for b2 in range(be, 4)}
                 rinv = 1.0 / rowcast(gs[be], e)
-                for q in range(2):
+                for q in TWO:
                     piv = rowcast(yv[be, q], e) * rinv
                     for b2 in range(be, 4):
                         new = yv[b2, q] - gs[b2] * piv
@@ -234,7 +243,7 @@
                             new = jnp.where(sub48 > e, new, jnp.where(sub48 == e, piv, yv[b2, q]))
                         yv[b2, q] = new
         for be in range(4):
-            for q in range(2):
+            for q in TWO:
                 ys[be, q] = yv[be, q].reshape(G6, 8, W)
 
     lane256 = lax.broadcasted_iota(jnp.int32, (8, T2), 1) % W
@@ -244,14 +253,14 @@
         for n in range(count):
             g = n
             rows = []
-            for p in range(2):
+            for p in TWO:
                 for m in range(8):
-                    for sg in range(2):
-                        parts = [jnp.where(grp == m, ys[2 * sg + p, q, g], 0.0) for q in range(2)]
+                    for sg in TWO:
+                        parts = [jnp.where(grp == m, ys[2 * sg + p, q, g], 0.0) for q in TWO]
                         rows.append(jnp.concatenate(parts, axis=1))
             dd.append(rows)
-            ll.append([jnp.concatenate([dl(half, g, q, p, m, sg) for q in range(2)], axis=1)
-                       for p in range(2) for m in range(8) for sg in range(2)])
+            ll.append([jnp.concatenate([dl(half, g, q, p, m, sg) for q in TWO], axis=1)
+                       for p in TWO for m in range(8) for sg in TWO])
         for h8 in (2, 4, 8):
             odd = [b for b in range(32) if (b % 16) // h8 % 2 == 1]
             zero = jnp.zeros((8, T2), F32)
@@ -275,7 +284,7 @@
         return remote(ref, ref, snd.at[0], misc_r.at[half], sid)
 
     def ltile(t):
-        return jnp.concatenate([lt[t, q].reshape(T2, W) for q in range(2)], axis=1)
+        return jnp.concatenate([lt[t, q].reshape(T2, W) for q in TWO], axis=1)
 
     need = [0, 1, 1, 0, 0, 1]
 
@@ -365,13 +374,14 @@
 
     def serve_c(n):
         cgot(n, 0, oy, k)
-        cput(n, 2, oy, sid).start()
+        cput(n, 1, oy, sid).start()
 
     def do_t(h):
         group = TG[h]
         for n in group:
-            cgot(n, 1, y, ok)
-            cgot(n, 2, oy, ok)
+            s, m0, m1 = CP[n]
+            both = c0.at[:, ok, 8 * s + m0:8 * s + m1]
+            remote(both, both, snd.at[0], crcv.at[n, 1], sid).wait_recv()
         lo = 8 * CP[group[0]][0] + CP[group[0]][1]
         hi = 8 * CP[group[-1]][0] + CP[group[-1]][2]
         g = 8 * (hi - lo)
@@ -379,9 +389,9 @@
             w = W * (u + 1)
             parts = []
             for j in (2 * u, 2 * u + 1):
-                for q in range(2):
+                for q in TWO:
                     parts.append(c0[q, :, lo:hi, :, W * j:W * j + W].reshape(2 * g, W))
-            rhs = jnp.concatenate([xa[2 * u + e, :, :, :, :, 0:w].reshape(T2, w) for e in range(2)], axis=0)
+            rhs = jnp.concatenate([xa[2 * u + e, :, :, :, :, 0:w].reshape(T2, w) for e in TWO], axis=0)
             d = dot(jnp.concatenate(parts, axis=1), rhs)
             if u:
                 acc[0:2 * g, 0:w - W] = acc[0:2 * g, 0:w - W] + d[:, 0:w - W]
@@ -390,7 +400,7 @@
             s, m0, m1 = CP[n]
             at = 8 * (8 * s + m0 - lo)
             size = 8 * (m1 - m0)
-            for p in range(2):
+            for p in TWO:
                 r = acc[p * g + at:p * g + at + size, 0:JW]
                 tt[s, p, m0:m1, x, :, :] = r.reshape(m1 - m0, 8, JW)
             tcopy(n, x).start()
@@ -404,7 +414,7 @@
         parts = []
         for e in range(nu):
             ln = pl.ds(pl.multiple_of((u + e) * W, W), W)
-            for q in range(2):
+            for q in TWO:
                 parts.append(bx[q, s:s + count, :, :, :, ln].reshape(count * W, W))
         rhs = jnp.concatenate([tt[u + e].reshape(T2, JW) for e in range(nu)], axis=0)
         return dot(jnp.concatenate(parts, axis=1), rhs)
@@ -478,7 +488,7 @@
     for n in range(NP):
         cput(n, 0, y, yid).wait_send()
         cput(n, 1, y, sid).wait_send()
-        cput(n, 2, oy, sid).wait_send()
+        cput(n, 1, oy, sid).wait_send()
         tcopy(n, x).wait_send()
     for s in range(6):
         bxcopy(s, k).wait_send()
@@ -504,8 +514,8 @@
             out_specs=pl.BlockSpec(memory_space=pl.ANY),
             scratch_shapes=[
                 vm(30, 2, 2, 8, 2, 8, W),
-                vm(2, 2, 2, 9, 4, 2, 8, W),
-                vm(2, 6, 4, 8, W),
+                vm(2, 2, 2, 30, 2, 8, W),
+                vm(2, 6, 6, 8, W),
                 vm(2, 2, 48, 8, HW),
                 vm(6, 2, 8, 2, 8, JW),
                 vm(6, 2, 8, 2, 8, HW),
@@ -519,7 +529,7 @@
                 vm(T2, HW),
                 vm(T2, JW),
                 vm(4, 2, 3, 8, W),
-                dma(NC + 1), dma(1), dma(NC, 7), dma(NP, 3), dma(NP), dma(6), dma(6), dma(6), dma(3), dma(1),
+                dma(NC + 1), dma(1), dma(NC, 4), dma(NP, 2), dma(NP), dma(6), dma(6), dma(6), dma(3), dma(1),
             ],
             compiler_params=pltpu.CompilerParams(
                 collective_id=0, has_side_effects=True, vmem_limit_bytes=47 * 2**20),

time: 81.2 us -> 79.5 us (0.979)
  Pallas kernels: 78.9 us -> 77.2 us
    pallas_call x1, Pallas kernels: 78.9 us -> 77.2 us  [body(): pl.pallas_call(kernel, name='tri_inverse', out_shape=jax.ShapeDtypeStruct...]
where the time goes in v5:
time: 79.5 us; the launch traced here: 79.4 us
  Pallas kernels  77.2 us (97%)
  local copies, waits for them, and re-layouts  2.19 us (3%)
    pallas_call x1, Pallas kernels, body(): pl.pallas_call(kernel, name='tri_inverse', out_shape=jax.ShapeDtypeStruct...  77.2 us
    unnamed x1, local copies, waits for them, and re-layouts  2.19 us

profile of v5, /device:TPU:0, one launch (start us, length us, event | category | flops | bytes accessed | tf_op | source)
XLA Modules:
  0.0 79.4 jit_solution(4254157298038945108)
XLA Ops:
  0.0 77.2 %tri_inverse.1 = f32[12,8,8,1536]{3,2,1,0:T(8,128)S(1)} custom-call(f32[96,8,1536]{2,1,0:T(8,128)} %bitcast.3), custom_call_target="tpu_custom_call" | custom-call | tf_op jit(solution)/shard_map/tri_inverse/pallas_call | solution.py:509
  77.2 2.2 %copy.3 = f32[768,1536]{1,0:T(8,128)} copy(f32[768,1536]{1,0:T(8,128)S(1)} %bitcast.2) | data formatting | bytes 9437184

commit v6 on v5

--- a/solution.py
+++ b/solution.py
@@ -16,29 +16,30 @@
 TIDX = {ij: t for t, ij in enumerate(TILES)}
 CHUNKS = [None, (0, 6), (6, 10), (10, 15), None, (15, 21), (21, 25), (25, 30)]
 NC = len(CHUNKS)
+YONLY = (1, 2, 3)
 NF, NG, ND, SIB = range(4)
 CP = [(0, 0, 8), (1, 0, 8), (2, 0, 8), (3, 0, 8), (4, 0, 8), (5, 0, 4), (5, 4, 8)]
 NP = len(CP)
 TG = [(0, 1), (2, 3), (4,), (5,), (6,)]
 ORDER = [
-    "f1 f4 f0 f2", "g0 c3 C0 F4", "g1 F0 c2 G0", "g3 f3 g2 g4", "G1 D0 f5 c5", "R0 F1 c4 F2",
-    "g5 I0 D4 F3", "G4 D1 R4 c0", "g6 c1 I1 Q0", "G2 f6 C1 V0", "R1 D2 F5 Q1", "G5 G3 C2 A1",
-    "A2 A3 R2 D3", "R3 f7 S0 c6", "C3 F6 C4 G6", "A4 V1 A5 D5", "T0 V2 R5 F7", "a0 C5 B1 D6",
-    "B2 V3 T1 V4", "B3 P0 R6 g7", "X0 T2 X1 B4", "Y1 P1 D7 C6", "V5 G7 X2 T3", "R7 V6 B5 Y2",
-    "o0 T4 X3 P2", "X4 X5 Y0 Y4", "Y3 Y5",
+    "g0 f0 c1 f2", "f1 f4 F0 c0", "f5 F2 f7 g5", "D0 G0 R0 I0", "F1 Q0 f3 R1", "E1 g4 F4 c5",
+    "A1 E2 C0 F5", "F3 A2 E3 C1", "G5 R2 A3 f6", "E4 G4 c4 g6", "D4 C2 R3 C3", "A4 V0 E5 F6",
+    "V1 c3 D5 R4", "G6 I1 A5 T0", "Q1 S0 C4 V2", "c2 R5 B1 D6", "V3 B2 P0 F7", "g7 T1 X0 B3",
+    "Y0 R6 a0 C5", "V4 B4 X1 D7", "T2 G7 P1 X2", "c6 C6 V5 R7", "B5 T3 V6 X3", "T4 P2 X4 X5",
+    "Y1 Y2 o0 Y4", "Y3 Y5",
 ]
-MODES = [2, 2, 3, 1, 1, 2, 2, 3]
+MODES = [2, 1, 3, 3, 0, 2, 1, 3]
 W, T2, JW, HW = 128, 256, 384, 768
 QW, HALF, SH = 32, 64, 24
-TWO = range(2)
+TWO, THREE, SIX = range(2), range(3), range(6)
 
 
 def dot(a, b):
     return jnp.dot(a, b, precision=lax.Precision.HIGHEST, preferred_element_type=F32)
 
 
-def kernel(l_hbm, out, lt, ld, raw, c0, xa, xb, bx, tt, db, oa, xc, oc, zz, acc, accx, ys,
-           loc, snd, rcv, crcv, trcv, orcv, brcv, bloc, misc_r, osem):
+def kernel(l_hbm, out, lt, ld, raw, ea, c0, xa, xb, bx, tt, db, oa, xc, oc, zz, acc, accx, ys,
+           loc, snd, rcv, crcv, trcv, orcv, brcv, bloc, misc_r, ercv, osem):
     row = lax.axis_index("row")
     y = lax.axis_index("col")
     x = row // 2
@@ -94,7 +95,7 @@
         if CHUNKS[c] is None:
             h = c // 4
             low, high = [], []
-            for n in range(6):
+            for n in SIX:
                 i = 6 * h + n
                 cols = slice(W * i, W * i + W)
                 low.append(pltpu.make_async_copy(l_hbm.at[8 * i:8 * i + 6, :, cols], raw.at[h, n], loc.at[c]))
@@ -134,18 +135,18 @@
             cp.wait()
         if copies and c < NC and CHUNKS[c] is None:
             h = c // 4
-            for n in range(6):
+            for n in SIX:
                 for e in TWO:
                     v = jnp.where(lane < W - QW, raw[h, n, 4 + e], turn(raw[h, n, e], QW))
                     ld[h, y, k, 4 * n + e, x] = v
-            for g in range(3):
+            for g in THREE:
                 for e in TWO:
                     v = jnp.where(lane < HALF, raw[h, 2 * g, 2 + e], turn(raw[h, 2 * g + 1, 2 + e], HALF))
                     ld[h, y, k, SH + 2 * g + e, x] = v
 
     def own_first(c):
         loaded(c)
-        put(c, NF, y, x, first(c))
+        put(c, NF, y, x, yid if c in YONLY else first(c))
         put(c, SIB, y, x, sid)
 
     def own_second(c):
@@ -170,6 +171,10 @@
         zz[...] = jnp.zeros(zz.shape, F32)
 
     def serve_f(c):
+        if c in YONLY:
+            got(c, NF, oy, k, x)
+            put(c, SIB, oy, x, sid)
+            return
         q, xs = from_first(c, k)
         got(c, NF, q, k, xs)
         put(c, ND, q, xs, second(c))
@@ -189,7 +194,7 @@
             ref = ld.at[c // 4, :, ok]
         else:
             lo, hi = CHUNKS[c]
-            ref = lt.at[lo:hi, :, ok]
+            ref = lt.at[lo:hi, :, ok, :, x] if c in YONLY else lt.at[lo:hi, :, ok]
         remote(ref, ref, snd.at[0], rcv.at[c, SIB], sid).wait_recv()
 
     G6 = 3
@@ -295,17 +300,29 @@
             d = db[i // 2, i % 2, :, pl.ds(pl.multiple_of(y * W, W), W)]
             xa[i, :, :, :, :, W * t:W * t + W] = d.reshape(2, 8, 2, 8, W)
 
-    def step_a(i):
+    def ecopy(i, xs):
+        n = W * ((i + 1) // 2)
+        ref = ea.at[i, :, :, xs, :, 0:n]
+        return remote(ref, ref, snd.at[0], ercv.at[i], xid)
+
+    def sum_a(i):
         for j in range(i):
             n = W * (j // 2 + 1)
-            d = dot(ltile(TIDX[i, j]), xa[j, :, :, :, :, 0:n].reshape(T2, n))
+            lhs = jnp.concatenate([lt[TIDX[i, j], q, :, :, x].reshape(W, W) for q in TWO], axis=1)
+            d = dot(lhs, xa[j, :, :, :, :, 0:n].reshape(T2, n))
             n0 = 0 if j == 0 else W * ((j - 1) // 2 + 1)
             if n0:
-                acc[:, 0:n0] = acc[:, 0:n0] + d[:, 0:n0]
+                acc[0:W, 0:n0] = acc[0:W, 0:n0] + d[:, 0:n0]
             if n > n0:
-                acc[:, n0:n] = d[:, n0:n]
+                acc[0:W, n0:n] = d[:, n0:n]
         n = W * ((i + 1) // 2)
-        r = -dot(db[i // 2, i % 2], acc[:, 0:n])
+        ea[i, :, :, x, :, 0:n] = acc[0:W, 0:n].reshape(2, 8, 8, n)
+        ecopy(i, x).start()
+
+    def step_a(i):
+        ecopy(i, ox).wait_recv()
+        n = W * ((i + 1) // 2)
+        r = -dot(db[i // 2, i % 2], ea[i, :, :, :, :, 0:n].reshape(T2, n))
         xa[i, :, :, :, :, 0:n] = r.reshape(2, 8, 2, 8, n)
         place_a(i)
 
@@ -342,14 +359,14 @@
 
     def finish_a():
         oacopy.start()
-        for i in range(6):
+        for i in SIX:
             put_out(zz, out.at[i, :, :, HW:2 * HW])
-        for t in range(3):
+        for t in THREE:
             put_out(xa.at[:, k, :, x, :, W * t:W * t + W], out.at[0:6, :, :, lanes(t, k)])
 
     def finish_oa():
         remote(oa, oa, snd.at[0], misc_r.at[2], sid).wait_recv()
-        for t in range(3):
+        for t in THREE:
             put_out(oa.at[:, :, :, W * t:W * t + W], out.at[0:6, :, :, lanes(t, ok)])
 
     def bxcopy(i, kk):
@@ -385,7 +402,7 @@
         lo = 8 * CP[group[0]][0] + CP[group[0]][1]
         hi = 8 * CP[group[-1]][0] + CP[group[-1]][2]
         g = 8 * (hi - lo)
-        for u in range(3):
+        for u in THREE:
             w = W * (u + 1)
             parts = []
             for j in (2 * u, 2 * u + 1):
@@ -444,12 +461,12 @@
         at = W * (s % 2)
         xc[s] = accx[at:at + W, :].reshape(2, 8, 8, JW)
         remote(xc.at[s, ok], oc.at[s], snd.at[0], orcv.at[s], sid).start()
-        for t in range(3):
+        for t in THREE:
             put_out(xc.at[s, k, :, :, W * t:W * t + W], out.at[6 + s, :, :, lanes(t, k)])
 
     def finish_x(s):
         remote(oc.at[s], oc.at[s], snd.at[0], orcv.at[s], sid).wait_recv()
-        for t in range(3):
+        for t in THREE:
             put_out(oc.at[s, :, :, W * t:W * t + W], out.at[6 + s, :, :, lanes(t, ok)])
 
     def inv(half):
@@ -473,7 +490,7 @@
         cput(n, 1, y, sid).start()
 
     run = {"f": own_first, "g": own_second, "F": serve_f, "G": serve_g, "D": serve_d, "R": ready, "I": inv,
-           "Q": get_d, "A": step_a, "B": do_b, "S": send_b, "C": csend, "c": csib, "V": serve_c, "T": do_t,
+           "Q": get_d, "A": step_a, "E": sum_a, "B": do_b, "S": send_b, "C": csend, "c": csib, "V": serve_c, "T": do_t,
            "X": do_x, "P": do_p, "Y": finish_x, "a": lambda _: finish_a(), "o": lambda _: finish_oa()}
     cleared = False
     for what, n in steps:
@@ -490,9 +507,11 @@
         cput(n, 1, y, sid).wait_send()
         cput(n, 1, oy, sid).wait_send()
         tcopy(n, x).wait_send()
-    for s in range(6):
+    for s in SIX:
         bxcopy(s, k).wait_send()
         remote(xc.at[s, ok], oc.at[s], snd.at[0], orcv.at[s], sid).wait_send()
+    for i in range(1, 6):
+        ecopy(i, x).wait_send()
     dbcopy(0, k).wait_send()
     dbcopy(1, k).wait_send()
     oacopy.wait_send()
@@ -516,6 +535,7 @@
                 vm(30, 2, 2, 8, 2, 8, W),
                 vm(2, 2, 2, 30, 2, 8, W),
                 vm(2, 6, 6, 8, W),
+                vm(6, 2, 8, 2, 8, JW),
                 vm(2, 2, 48, 8, HW),
                 vm(6, 2, 8, 2, 8, JW),
                 vm(6, 2, 8, 2, 8, HW),
@@ -529,7 +549,7 @@
                 vm(T2, HW),
                 vm(T2, JW),
                 vm(4, 2, 3, 8, W),
-                dma(NC + 1), dma(1), dma(NC, 4), dma(NP, 2), dma(NP), dma(6), dma(6), dma(6), dma(3), dma(1),
+                dma(NC + 1), dma(1), dma(NC, 4), dma(NP, 2), dma(NP), dma(6), dma(6), dma(6), dma(3), dma(6), dma(1),
             ],
             compiler_params=pltpu.CompilerParams(
                 collective_id=0, has_side_effects=True, vmem_limit_bytes=47 * 2**20),

time: 79.5 us -> 78.1 us (0.982)
  Pallas kernels: 77.2 us -> 75.8 us
    pallas_call x1, Pallas kernels: 77.2 us -> 75.8 us  [body(): pl.pallas_call(kernel, name='tri_inverse', out_shape=jax.ShapeDtypeStruct...]
where the time goes in v6:
time: 78.1 us; the launch traced here: 78 us
  Pallas kernels  75.8 us (97%)
  local copies, waits for them, and re-layouts  2.19 us (3%)
    pallas_call x1, Pallas kernels, body(): pl.pallas_call(kernel, name='tri_inverse', out_shape=jax.ShapeDtypeStruct...  75.8 us
    unnamed x1, local copies, waits for them, and re-layouts  2.19 us

profile of v6, /device:TPU:0, one launch (start us, length us, event | category | flops | bytes accessed | tf_op | source)
XLA Modules:
  0.0 78.0 jit_solution(6335772374885501454)
XLA Ops:
  0.0 75.8 %tri_inverse.1 = f32[12,8,8,1536]{3,2,1,0:T(8,128)S(1)} custom-call(f32[96,8,1536]{2,1,0:T(8,128)} %bitcast.3), custom_call_target="tpu_custom_call" | custom-call | tf_op jit(solution)/shard_map/tri_inverse/pallas_call | solution.py:528
  75.8 2.2 %copy.3 = f32[768,1536]{1,0:T(8,128)} copy(f32[768,1536]{1,0:T(8,128)S(1)} %bitcast.2) | data formatting | bytes 9437184

commit v7 on v6

--- a/solution.py
+++ b/solution.py
@@ -22,13 +22,13 @@
 NP = len(CP)
 TG = [(0, 1), (2, 3), (4,), (5,), (6,)]
 ORDER = [
-    "g0 f0 c1 f2", "f1 f4 F0 c0", "f5 F2 f7 g5", "D0 G0 R0 I0", "F1 Q0 f3 R1", "E1 g4 F4 c5",
-    "A1 E2 C0 F5", "F3 A2 E3 C1", "G5 R2 A3 f6", "E4 G4 c4 g6", "D4 C2 R3 C3", "A4 V0 E5 F6",
-    "V1 c3 D5 R4", "G6 I1 A5 T0", "Q1 S0 C4 V2", "c2 R5 B1 D6", "V3 B2 P0 F7", "g7 T1 X0 B3",
-    "Y0 R6 a0 C5", "V4 B4 X1 D7", "T2 G7 P1 X2", "c6 C6 V5 R7", "B5 T3 V6 X3", "T4 P2 X4 X5",
-    "Y1 Y2 o0 Y4", "Y3 Y5",
+    "g0 f0 f1 f3", "f4 G0 c0 F0", "D0 g5 R0 f7", "f2 I0 F1 f5", "Q0 g4 C0 C1", "c2 F3 R1 E1",
+    "R3 F4 F2 A1", "E2 R2 F5 A2", "E3 A3 c5 f6", "E4 c1 C2 g6", "G4 G5 V0 D4", "D5 A4 E5 C3",
+    "V1 R5 F6 R4", "c3 c4 g7 I1", "V2 A5 T0 C4", "G6 V3 Q1 S0", "D6 B1 T1 c6", "B2 R6 a0 B3",
+    "C5 G7 V4 F7", "B4 P0 X0 X1", "V5 T2 C6 P1", "D7 Y0 T3 o0", "X2 V6 R7 B5", "X3 T4 P2 X4",
+    "X5 Y4 Y1 Y3", "Y2 Y5",
 ]
-MODES = [2, 1, 3, 3, 0, 2, 1, 3]
+MODES = [2, 2, 0, 3, 1, 2, 1, 3]
 W, T2, JW, HW = 128, 256, 384, 768
 QW, HALF, SH = 32, 64, 24
 TWO, THREE, SIX = range(2), range(3), range(6)

time: 78.1 us -> 77.7 us (level)
  no operation moved by 1% of the time
where the time goes in v7:
time: 77.7 us; the launch traced here: 77.6 us
  Pallas kernels  75.4 us (97%)
  local copies, waits for them, and re-layouts  2.19 us (3%)
    pallas_call x1, Pallas kernels, body(): pl.pallas_call(kernel, name='tri_inverse', out_shape=jax.ShapeDtypeStruct...  75.4 us
    unnamed x1, local copies, waits for them, and re-layouts  2.19 us

profile of v7, /device:TPU:0, one launch (start us, length us, event | category | flops | bytes accessed | tf_op | source)
XLA Modules:
  0.0 77.6 jit_solution(6753203970460895665)
XLA Ops:
  0.0 75.4 %tri_inverse.1 = f32[12,8,8,1536]{3,2,1,0:T(8,128)S(1)} custom-call(f32[96,8,1536]{2,1,0:T(8,128)} %bitcast.3), custom_call_target="tpu_custom_call" | custom-call | tf_op jit(solution)/shard_map/tri_inverse/pallas_call | solution.py:528
  75.4 2.2 %copy.3 = f32[768,1536]{1,0:T(8,128)} copy(f32[768,1536]{1,0:T(8,128)S(1)} %bitcast.2) | data formatting | bytes 9437184
